TPU v7x, 16 devices: a whole 2x2x2 slice. The times are simulated.
16 devices in a mesh: cp: 2 (over z), fsdp: 8 (over y, x, core).
Axes of the slice: x: 2, y: 2, z: 2, core: 2. Of those that a mesh axis runs over, the one named last changes fastest.
Arguments:
- hidden: bfloat16 [48, 512, 1536], P('fsdp', 'cp')
- tok_pos: int32 [48, 512], P('fsdp', 'cp')
- grad_out: bfloat16 [48, 512, 1536], P('fsdp', 'cp')
- norm_gain: float32 [1536], P(('fsdp', 'cp'))
- w_query: bfloat16 [1536, 1536], P(('fsdp', 'cp'))
- w_key: bfloat16 [1536, 256], P(('fsdp', 'cp'))
- w_value: bfloat16 [1536, 256], P(('fsdp', 'cp'))
- w_out: bfloat16 [1536, 1536], P(('fsdp', 'cp'))
Outputs:
- output 1: bfloat16 [48, 512, 1536], P('fsdp', 'cp')
- output 2: bfloat16 [48, 512, 1536], P('fsdp', 'cp')
- output 3: float32 [1536, 1536], P(('fsdp', 'cp'))
- output 4: float32 [1536, 256], P(('fsdp', 'cp'))
- output 5: float32 [1536, 256], P(('fsdp', 'cp'))
- output 6: float32 [1536, 1536], P(('fsdp', 'cp'))
- output 7: float32 [1536], P(('fsdp', 'cp'))
All inputs are finite; a program needn't handle non-finite values.
Results may differ from a plain program's by a relative error of at most 0.00682371.
Values are sent between devices in bfloat16 or wider.
A program may use at most 1 GiB of HBM per device.

v0:
```python
import functools
import math

import jax
import jax.numpy as jnp
from jax import lax
from jax.experimental import pallas as pl
from jax.experimental.pallas import tpu as pltpu
from jax.sharding import PartitionSpec as P

HEAD = 128
THETA = 1000000.0
EPS = 1e-5
NEG = -1e30
SCALE = HEAD ** -0.5
LOG2E = math.log2(math.e)
AXES = ('fsdp', 'cp')
MESH = pl.DeviceIdType.MESH
F32 = jnp.float32
BF16 = jnp.bfloat16
NT = (((1,), (1,)), ((), ()))
TN = (((0,), (0,)), ((), ()))
NN = (((1,), (0,)), ((), ()))


def dot(a, b, dims=NN):
    return lax.dot_general(a, b, dims, preferred_element_type=F32)


def rope(v, cos2, sin2):
    return v * cos2 + pltpu.roll(v, HEAD // 2, 1) * sin2


def unrope(v, cos2, sin2):
    return v * cos2 - pltpu.roll(v, HEAD // 2, 1) * sin2


def attn_kernel(n_seq, rows, groups, gsize,
                q_ref, do_ref, kvo_ref, kvx_ref, pq_ref, pk_ref, px_ref, cos_ref, sin_ref,
                o_ref, dq_ref, dkv_ref,
                mask, p_s, ds_s, own, snd, rcv, send_sem, recv_sem):
    step = pl.program_id(0)
    n_steps = n_seq * groups
    seq = step // groups
    grp = step % groups
    cp = lax.axis_index('cp')
    peer = {'cp': 1 - cp}

    @pl.when(step == 0)
    def _():
        barrier = pltpu.get_barrier_semaphore()
        pl.semaphore_signal(barrier, inc=1, device_id=peer, device_id_type=MESH)
        pl.semaphore_wait(barrier, 1)

    @pl.when(grp == 0)
    def _():
        pq = pq_ref[...]
        mask[:, :rows] = jnp.where(pk_ref[0] <= pq, 0.0, NEG)
        mask[:, rows:] = jnp.where(px_ref[0] <= pq, 0.0, NEG)

    row0 = pl.multiple_of(seq * rows, rows)
    cos2 = cos_ref[pl.ds(row0, rows), :]
    sin2 = sin_ref[pl.ds(row0, rows), :]
    k = jnp.concatenate([kvo_ref[:, :HEAD], kvx_ref[:, :HEAD]], axis=0)
    v = jnp.concatenate([kvo_ref[:, HEAD:], kvx_ref[:, HEAD:]], axis=0)
    for h in range(gsize):
        cols = slice(h * HEAD, (h + 1) * HEAD)
        hrow = slice(h * rows, (h + 1) * rows)
        q = q_ref[:, cols]
        do = do_ref[:, cols]
        s = dot(q, k, NT) * (SCALE * LOG2E) + mask[...]
        m = jnp.max(s, axis=1, keepdims=True)
        e = jnp.exp2(s - m)
        l = jnp.sum(e, axis=1, keepdims=True)
        rl = 1.0 / l
        o = (dot(e.astype(BF16), v) * rl).astype(BF16)
        o_ref[:, cols] = o
        delta = jnp.sum(do.astype(F32) * o.astype(F32), axis=1, keepdims=True)
        p = e * rl
        p_s[hrow, :] = p.astype(BF16)
        ds = (p * (dot(do, v, NT) - delta)).astype(BF16)
        ds_s[hrow, :] = ds
        dq_ref[:, cols] = unrope(dot(ds, k) * SCALE, cos2, sin2).astype(BF16)
    do6 = jnp.concatenate([do_ref[:, h * HEAD:(h + 1) * HEAD] for h in range(gsize)], axis=0)
    q6 = jnp.concatenate([q_ref[:, h * HEAD:(h + 1) * HEAD] for h in range(gsize)], axis=0)
    dv = dot(p_s[...], do6, TN)
    dk = dot(ds_s[...], q6, TN) * SCALE
    own[step, :, :HEAD] = dk[:rows]
    own[step, :, HEAD:] = dv[:rows]
    snd[step, :, :HEAD] = dk[rows:]
    snd[step, :, HEAD:] = dv[rows:]

    def copy(i):
        return pltpu.make_async_remote_copy(snd.at[i], rcv.at[i], send_sem.at[i], recv_sem.at[i],
                                            device_id=peer, device_id_type=MESH)

    copy(step).start()

    @pl.when(step == n_steps - 1)
    def _():
        def fin(i, carry):
            copy(i).wait()
            r0 = pl.multiple_of((i // groups) * rows, rows)
            tot = own[i] + rcv[i]
            c2 = cos_ref[pl.ds(r0, rows), :]
            s2 = sin_ref[pl.ds(r0, rows), :]
            dkv_ref[i, :, :HEAD] = unrope(tot[:, :HEAD], c2, s2).astype(BF16)
            dkv_ref[i, :, HEAD:] = tot[:, HEAD:].astype(BF16)
            return carry
        lax.fori_loop(0, n_steps, fin, 0)


def attention(q, do, kv_own, kv_oth, pos, pos_oth, cos2, sin2):
    n_seq, rows = pos.shape
    groups = kv_own.shape[1] // (2 * HEAD)
    gsize = q.shape[1] // HEAD // groups
    steps = n_seq * groups
    gcols = gsize * HEAD
    tokens = n_seq * rows
    blk = lambda c: pl.BlockSpec((rows, c), lambda i: (i // groups, i % groups))
    row3 = pl.BlockSpec((1, 1, rows), lambda i: (i // groups, 0, 0))
    full = lambda *s: pl.BlockSpec(s, lambda i: (0,) * len(s))
    o, dq, dkv = pl.pallas_call(
        functools.partial(attn_kernel, n_seq, rows, groups, gsize),
        grid=(steps,),
        in_specs=[blk(gcols), blk(gcols), blk(2 * HEAD), blk(2 * HEAD),
                  pl.BlockSpec((rows, 1), lambda i: (i // groups, 0)), row3, row3,
                  full(tokens, HEAD), full(tokens, HEAD)],
        out_specs=[blk(gcols), blk(gcols), full(steps, rows, 2 * HEAD)],
        out_shape=[jax.ShapeDtypeStruct(q.shape, BF16), jax.ShapeDtypeStruct(q.shape, BF16),
                   jax.ShapeDtypeStruct((steps, rows, 2 * HEAD), BF16)],
        scratch_shapes=[
            pltpu.VMEM((rows, 2 * rows), F32),
            pltpu.VMEM((gsize * rows, 2 * rows), BF16),
            pltpu.VMEM((gsize * rows, 2 * rows), BF16),
            pltpu.VMEM((steps, rows, 2 * HEAD), F32),
            pltpu.VMEM((steps, rows, 2 * HEAD), F32),
            pltpu.VMEM((steps, rows, 2 * HEAD), F32),
            pltpu.SemaphoreType.DMA((steps,)),
            pltpu.SemaphoreType.DMA((steps,)),
        ],
        compiler_params=pltpu.CompilerParams(
            collective_id=0, has_side_effects=True, dimension_semantics=('arbitrary',),
            vmem_limit_bytes=60 * 2 ** 20),
        cost_estimate=pl.CostEstimate(flops=2 * 7 * tokens * 2 * rows * gcols * groups,
                                      bytes_accessed=24 * 2 ** 20, transcendentals=0),
    )(q, do, kv_own, kv_oth, pos.reshape(tokens, 1), pos[:, None, :], pos_oth, cos2, sin2)
    return o, dq, dkv.reshape(n_seq, groups, rows, 2, HEAD)

COLORS = ('xyz', 'yzx', 'zxy')


def place():
    f = lax.axis_index('fsdp')
    z = lax.axis_index('cp')
    bits = {'y': f // 4, 'x': (f // 2) % 2, 'c': f % 2, 'z': z}
    peers = {'y': {'fsdp': f + 4 - 8 * bits['y']}, 'x': {'fsdp': f + 2 - 4 * bits['x']},
             'c': {'fsdp': f + 1 - 2 * bits['c']}, 'z': {'cp': 1 - z}}
    return bits, peers


def meet(peers):
    barrier = pltpu.get_barrier_semaphore()
    for a in 'cxyz':
        pl.semaphore_signal(barrier, inc=1, device_id=peers[a], device_id_type=MESH)
    pl.semaphore_wait(barrier, 4)


def wgrad_kernel(shapes, o_hbm, dy_hbm, r_hbm, dq_hbm, dkv_hbm, gp_ref,
                 gin_ref, gwo_ref, gg_ref,
                 lhs, rhs, g, rcv_a, h, rcv1, rcv2, rcv3, gain_rcv,
                 load_sem, d2d_send, d2d_recv, ici_send, ici_recv, gain_send, gain_recv, credit):
    tokens, dim, width, sub = shapes
    bits, peers = place()
    core = bits['c']
    chunks = [(0, dy_hbm, j, gwo_ref, j) for j in range(dim // width)]
    chunks += [(1, dq_hbm, j, gin_ref, j) for j in range(dim // width)]
    chunks += [(1, dkv_hbm, 0, gin_ref, dim // width)]
    n = len(chunks)
    seg = dim // 4
    half = seg // 2

    def load_lhs(i):
        return pltpu.make_async_copy((o_hbm, r_hbm)[i], lhs.at[i], load_sem.at[i])

    def load_rhs(t):
        src, j = chunks[t][1], chunks[t][2]
        return pltpu.make_async_copy(src.at[:, pl.ds(j * width, width)], rhs.at[t % 2], load_sem.at[2 + t])

    load_lhs(0).start()
    load_rhs(0).start()
    load_lhs(1).start()
    load_rhs(1).start()
    meet(peers)

    def d2d(t):
        return pltpu.make_async_remote_copy(g.at[t % 2, :, 1 - core], rcv_a.at[t % 2], d2d_send.at[t], d2d_recv.at[t],
                                            device_id=peers['c'], device_id_type=MESH)

    def ici(t, c, p):
        b1, b2, b3 = (bits[a] for a in COLORS[c])
        if p == 0:
            src, dst = h.at[t, c, pl.ds((1 - b1) * 4, 4)], rcv1.at[t, c]
        elif p == 1:
            src, dst = h.at[t, c, pl.ds(b1 * 4 + (1 - b2) * 2, 2)], rcv2.at[t, c]
        else:
            src, dst = h.at[t, c, pl.ds(b1 * 4 + b2 * 2 + (1 - b3), 1)], rcv3.at[t, c]
        return pltpu.make_async_remote_copy(src, dst, ici_send.at[t, c, p], ici_recv.at[t, c, p],
                                            device_id=peers[COLORS[c][p]], device_id_type=MESH)

    def compute(t):
        li = chunks[t][0]
        if t == 0 or chunks[t - 1][0] != li:
            load_lhs(li).wait()
        load_rhs(t).wait()

        def body(yx, carry):
            cols = pl.ds(pl.multiple_of(yx * seg, HEAD), seg)
            res = dot(lhs[li, :, cols], rhs[t % 2], TN)
            g[t % 2, yx, 0] = res[:half]
            g[t % 2, yx, 1] = res[half:]
            return carry
        lax.fori_loop(0, 4, body, 0)
        if t + 2 < n:
            load_rhs(t + 2).start()
        if t >= 2:
            pl.semaphore_wait(credit, 1)
        d2d(t).start()

    def fold(t):
        d2d(t).wait()
        for y in range(2):
            for x in range(2):
                for z in range(2):
                    at = {'y': y, 'x': x, 'z': z}
                    for c in range(3):
                        a1, a2, a3 = (at[a] for a in COLORS[c])
                        rows = slice(z * 3 * sub + c * sub, z * 3 * sub + (c + 1) * sub)
                        h[t, c, a1 * 4 + a2 * 2 + a3] = g[t % 2, y * 2 + x, core, rows] + rcv_a[t % 2, y * 2 + x, rows]
        for c in range(3):
            ici(t, c, 0).start()
        if t + 2 < n:
            pl.semaphore_signal(credit, inc=1, device_id=peers['c'], device_id_type=MESH)

    def reduce(t, p):
        for c in range(3):
            b1, b2, b3 = (bits[a] for a in COLORS[c])
            ici(t, c, p).wait()
            if p == 0:
                for j in range(4):
                    h[t, c, b1 * 4 + j] = h[t, c, b1 * 4 + j] + rcv1[t, c, j]
                ici(t, c, 1).start()
            elif p == 1:
                for j in range(2):
                    k = b1 * 4 + b2 * 2 + j
                    h[t, c, k] = h[t, c, k] + rcv2[t, c, j]
                ici(t, c, 2).start()
            else:
                out, j = chunks[t][3], chunks[t][4]
                k = b1 * 4 + b2 * 2 + b3
                out[c * sub:(c + 1) * sub, j * width:(j + 1) * width] = h[t, c, k] + rcv3[t, c, 0]

    gg_ref[...] = gp_ref[...]

    def gain_copy(i):
        return pltpu.make_async_remote_copy(gg_ref, gain_rcv.at[i], gain_send.at[i], gain_recv.at[i],
                                            device_id=peers['cxyz'[i]], device_id_type=MESH)

    gain_copy(0).start()
    for i in range(n + 4):
        if i < n:
            compute(i)
        if 0 <= i - 1 < n:
            fold(i - 1)
        if i < 4:
            gain_copy(i).wait()
            gg_ref[...] = gg_ref[...] + gain_rcv[i]
            if i < 3:
                gain_copy(i + 1).start()
        for p in range(3):
            if 0 <= i - 2 - p < n:
                reduce(i - 2 - p, p)


def wgrad(o, dy, r, dq, dkv, gp):
    tokens, dim = o.shape
    width = dkv.shape[1]
    shard = dim // 16
    sub = shard // 3
    n = 2 * (dim // width) + 1
    hbm = pl.BlockSpec(memory_space=pl.ANY)
    vm = pl.BlockSpec(memory_space=pltpu.VMEM)
    dma = pltpu.SemaphoreType.DMA
    return pl.pallas_call(
        functools.partial(wgrad_kernel, (tokens, dim, width, sub)),
        in_specs=[hbm] * 5 + [vm],
        out_specs=[vm] * 3,
        out_shape=[jax.ShapeDtypeStruct((shard, dim + width), F32), jax.ShapeDtypeStruct((shard, dim), F32),
                   jax.ShapeDtypeStruct((1, dim), F32)],
        scratch_shapes=[
            pltpu.VMEM((2, tokens, dim), BF16),
            pltpu.VMEM((2, tokens, width), BF16),
            pltpu.VMEM((2, 4, 2, dim // 8, width), F32),
            pltpu.VMEM((2, 4, dim // 8, width), F32),
            pltpu.VMEM((n, 3, 8, sub, width), F32),
            pltpu.VMEM((n, 3, 4, sub, width), F32),
            pltpu.VMEM((n, 3, 2, sub, width), F32),
            pltpu.VMEM((n, 3, 1, sub, width), F32),
            pltpu.VMEM((4, 1, dim), F32),
            dma((2 + n,)), dma((n,)), dma((n,)), dma((n, 3, 3)), dma((n, 3, 3)), dma((4,)), dma((4,)),
            pltpu.SemaphoreType.REGULAR,
        ],
        compiler_params=pltpu.CompilerParams(collective_id=1, has_side_effects=True, vmem_limit_bytes=60 * 2 ** 20),
        cost_estimate=pl.CostEstimate(flops=2 * tokens * dim * (2 * dim + width), bytes_accessed=30 * 2 ** 20,
                                      transcendentals=0),
    )(o, dy, r, dq, dkv, gp)


def gather_kernel(shapes, x_hbm, dy_hbm, wq_hbm, wk_hbm, wv_hbm, wo_hbm, gain_ref, pcol_ref, prow_ref, freq_ref,
                  q_hbm, do_hbm, r_hbm, kvo_hbm, kvx_hbm, wi_hbm, wf_hbm, cos_ref, sin_ref, gain_out, px_out,
                  x, dy, r, q, do, kvo, kvx, wi, wo, gbuf, grow, px,
                  load_sem, out_sem, ici_send, ici_recv, fwd_send, fwd_recv, own_send, own_recv,
                  g_send, g_recv, kv_send, kv_recv):
    n_seq, rows, dim, n_kv = shapes
    bits, peers = place()
    by, bx, bc, bz = (bits[a] for a in 'yxcz')
    shard = dim // 16
    third, mid = shard // 3, shard // 2
    fast = [(a, slice(i * third, (i + 1) * third)) for i, a in enumerate(COLORS)]
    slim = [(a, slice(i * mid, (i + 1) * mid)) for i, a in enumerate(('zxy', 'zyx'))]
    hq = dim // 2
    pieces = [(wi, slice(dim, dim + 2 * n_kv), fast), (wo, slice(0, dim), slim),
              (wi, slice(0, hq), slim), (wi, slice(hq, dim), slim)]

    loads = []

    def load(src, dst):
        c = pltpu.make_async_copy(src, dst, load_sem.at[len(loads)])
        c.start()
        loads.append(c)
        return len(loads) - 1

    mine = lambda ref, cols: ref.at[by, bx, bc, bz, :, cols]
    for g in range(n_kv // HEAD):
        hc = slice(g * HEAD, (g + 1) * HEAD)
        load(wk_hbm.at[:, hc], mine(wi, slice(dim + 2 * g * HEAD, dim + (2 * g + 1) * HEAD)))
        load(wv_hbm.at[:, hc], mine(wi, slice(dim + (2 * g + 1) * HEAD, dim + (2 * g + 2) * HEAD)))
    n_first = len(loads)
    l_o = load(wo_hbm, mine(wo, slice(0, dim)))
    l_q = load(wq_hbm, mine(wi, slice(0, dim)))
    l_x = load(x_hbm, x)
    l_dy = load(dy_hbm, dy)
    gbuf[by, bx, bc, bz] = gain_ref[...]
    meet(peers)

    def region(p, c, f, flip):
        ref, cols, colors = pieces[p]
        order, rws = colors[c]
        idx = []
        for a in 'yxcz':
            if a in order[:f]:
                idx.append(slice(None))
            elif a == order[f] and flip:
                idx.append(1 - bits[a])
            else:
                idx.append(bits[a])
        return ref.at[idx[0], idx[1], idx[2], idx[3], rws, cols]

    def ici(p, c, f):
        s = region(p, c, f, False)
        return pltpu.make_async_remote_copy(s, s, ici_send.at[p, c, f], ici_recv.at[p, c, f],
                                            device_id=peers[pieces[p][2][c][0][f]], device_id_type=MESH)

    def fwd(p, c, f):
        s = region(p, c, f, True)
        return pltpu.make_async_remote_copy(s, s, fwd_send.at[p, c, f], fwd_recv.at[p, c, f],
                                            device_id=peers['c'], device_id_type=MESH)

    def own(p):
        s = mine(pieces[p][0], pieces[p][1])
        return pltpu.make_async_remote_copy(s, s, own_send.at[p], own_recv.at[p],
                                            device_id=peers['c'], device_id_type=MESH)

    def begin(p):
        for c in range(len(pieces[p][2])):
            ici(p, c, 0).start()
        own(p).start()

    def advance(p, f):
        for c in range(len(pieces[p][2])):
            ici(p, c, f).wait()
            if f < 2:
                ici(p, c, f + 1).start()
            fwd(p, c, f).start()

    def settle(p):
        own(p).wait()
        for c in range(len(pieces[p][2])):
            for f in range(3):
                fwd(p, c, f).wait()

    def gain_copy(i):
        s = (gbuf.at[by, bx, bc, bz], gbuf.at[by, bx, :, bz], gbuf.at[by, bx], gbuf.at[by])[i]
        return pltpu.make_async_remote_copy(s, s, g_send.at[i], g_recv.at[i],
                                            device_id=peers['czxy'[i]], device_id_type=MESH)

    def kv_copy(i):
        return pltpu.make_async_remote_copy(kvo.at[i], kvx.at[i], kv_send.at[i], kv_recv.at[i],
                                            device_id=peers['z'], device_id_type=MESH)

    def px_copy():
        return pltpu.make_async_remote_copy(prow_ref, px, kv_send.at[n_seq], kv_recv.at[n_seq],
                                            device_id=peers['z'], device_id_type=MESH)

    gain_copy(0).start()
    for i in range(n_first):
        loads[i].wait()
    begin(0)
    px_copy().start()
    loads[l_o].wait()
    begin(1)
    loads[l_q].wait()
    begin(2)
    begin(3)
    gain_copy(0).wait()
    gain_copy(1).start()

    def tables(i, carry):
        rs = pl.ds(pl.multiple_of(i * rows, rows), rows)
        ang = pcol_ref[rs, :].astype(F32) * freq_ref[...]
        lane = lax.broadcasted_iota(jnp.int32, (rows, HEAD), 1)
        cos_ref[rs, :] = jnp.cos(ang)
        sn = jnp.sin(ang)
        sin_ref[rs, :] = jnp.where(lane < HEAD // 2, -sn, sn)
        return carry

    lax.fori_loop(0, n_seq // 2, tables, 0)
    gain_copy(1).wait()
    gain_copy(2).start()
    advance(0, 0)
    lax.fori_loop(n_seq // 2, n_seq, tables, 0)
    gain_copy(2).wait()
    gain_copy(3).start()
    advance(0, 1)
    gain_copy(3).wait()
    lane = lax.broadcasted_iota(jnp.int32, (8, HEAD), 1)
    for b in range(dim // HEAD):
        acc = jnp.zeros((8, HEAD), F32)
        for sh in range(16):
            lo = shard * sh - HEAD * b
            if lo >= HEAD or lo + shard <= 0:
                continue
            row = jnp.broadcast_to(gbuf[sh // 8, (sh // 4) % 2, (sh // 2) % 2, sh % 2], (8, HEAD))
            row = pltpu.roll(row, lo % HEAD, 1) if lo % HEAD else row
            acc = jnp.where((lane >= lo) & (lane < lo + shard), row, acc)
        grow[:, b * HEAD:(b + 1) * HEAD] = acc
    gain_out[...] = grow[0:1, :]
    loads[l_x].wait()

    def norm(i, carry):
        rs = pl.ds(pl.multiple_of(i * rows // 2, rows // 2), rows // 2)
        xf = x[rs, :].astype(F32)
        inv = lax.rsqrt(jnp.mean(xf * xf, axis=1, keepdims=True) + EPS)
        r[rs, :] = (xf * inv * grow[0:1, :]).astype(BF16)
        return carry

    lax.fori_loop(0, 2 * n_seq, norm, 0)
    r_out = pltpu.make_async_copy(r, r_hbm, out_sem.at[0])
    r_out.start()
    advance(0, 2)
    advance(1, 0)
    settle(0)

    def kv_proj(i, carry):
        rs = pl.ds(pl.multiple_of(i * rows, rows), rows)
        w = wi[:, :, :, :, :, dim:dim + 2 * n_kv].reshape(dim, 2 * n_kv)
        kv = dot(r[rs, :], w)
        for g in range(n_kv // HEAD):
            kc = slice(2 * g * HEAD, (2 * g + 1) * HEAD)
            vc = slice((2 * g + 1) * HEAD, (2 * g + 2) * HEAD)
            kvo[i, :, kc] = rope(kv[:, kc], cos_ref[rs, :], sin_ref[rs, :]).astype(BF16)
            kvo[i, :, vc] = kv[:, vc].astype(BF16)
        kv_copy(i).start()
        return carry

    lax.fori_loop(0, n_seq, kv_proj, 0)
    kvo_out = pltpu.make_async_copy(kvo, kvo_hbm, out_sem.at[1])
    kvo_out.start()
    advance(1, 1)
    advance(2, 0)
    advance(1, 2)
    settle(1)
    loads[l_dy].wait()

    def do_proj(i, carry):
        rs = pl.ds(pl.multiple_of(i * rows, rows), rows)
        do[rs, :] = dot(dy[rs, :], wo[...].reshape(dim, dim), NT).astype(BF16)
        return carry

    def q_proj(half):
        def body(i, carry):
            rs = pl.ds(pl.multiple_of(i * rows, rows), rows)
            res = dot(r[rs, :], wi[:, :, :, :, :, half * hq:(half + 1) * hq].reshape(dim, hq))
            for h in range(hq // HEAD):
                hc = slice(h * HEAD, (h + 1) * HEAD)
                q[rs, half * hq + h * HEAD:half * hq + (h + 1) * HEAD] = rope(
                    res[:, hc], cos_ref[rs, :], sin_ref[rs, :]).astype(BF16)
            return carry
        return body

    lax.fori_loop(0, n_seq // 2, do_proj, 0)
    advance(2, 1)
    advance(3, 0)
    lax.fori_loop(n_seq // 2, n_seq, do_proj, 0)
    do_out = pltpu.make_async_copy(do, do_hbm, out_sem.at[2])
    do_out.start()
    wf_out = pltpu.make_async_copy(wo, wf_hbm, out_sem.at[3])
    wf_out.start()
    advance(2, 2)
    advance(3, 1)
    settle(2)
    lax.fori_loop(0, n_seq, q_proj(0), 0)
    advance(3, 2)
    settle(3)
    wi_out = pltpu.make_async_copy(wi, wi_hbm, out_sem.at[4])
    wi_out.start()
    lax.fori_loop(0, n_seq, q_proj(1), 0)
    q_out = pltpu.make_async_copy(q, q_hbm, out_sem.at[5])
    q_out.start()
    px_copy().wait()
    px_out[...] = px[...]
    for i in range(n_seq):
        kv_copy(i).wait()
    kvx_out = pltpu.make_async_copy(kvx, kvx_hbm, out_sem.at[6])
    kvx_out.start()
    for c in (r_out, kvo_out, do_out, wf_out, wi_out, q_out, kvx_out):
        c.wait()


def gather_project(x, dy, wq, wk, wv, wo, gain, pos):
    tokens, dim = x.shape
    n_seq, rows = pos.shape
    n_kv = wk.shape[1]
    shard = dim // 16
    half = HEAD // 2
    freq = THETA ** (-jnp.arange(half, dtype=F32) / half)
    freq = jnp.concatenate([freq, freq])[None]
    gain = jnp.pad(gain, (0, HEAD - shard))[None]
    hbm = pl.BlockSpec(memory_space=pl.ANY)
    vm = pl.BlockSpec(memory_space=pltpu.VMEM)
    dma = pltpu.SemaphoreType.DMA
    sds = jax.ShapeDtypeStruct
    wshape = (2, 2, 2, 2, shard)
    return pl.pallas_call(
        functools.partial(gather_kernel, (n_seq, rows, dim, n_kv)),
        in_specs=[hbm] * 6 + [vm] * 4,
        out_specs=[hbm] * 7 + [vm] * 4,
        out_shape=[sds((tokens, dim), BF16), sds((tokens, dim), BF16), sds((tokens, dim), BF16),
                   sds((n_seq, rows, 2 * n_kv), BF16), sds((n_seq, rows, 2 * n_kv), BF16),
                   sds(wshape + (dim + 2 * n_kv,), BF16), sds(wshape + (dim,), BF16),
                   sds((tokens, HEAD), F32), sds((tokens, HEAD), F32), sds((1, dim), F32),
                   sds((n_seq, 1, rows), jnp.int32)],
        scratch_shapes=[pltpu.VMEM((tokens, dim), BF16)] * 5 + [
            pltpu.VMEM((n_seq, rows, 2 * n_kv), BF16),
            pltpu.VMEM((n_seq, rows, 2 * n_kv), BF16),
            pltpu.VMEM(wshape + (dim + 2 * n_kv,), BF16),
            pltpu.VMEM(wshape + (dim,), BF16),
            pltpu.VMEM((2, 2, 2, 2, 1, HEAD), F32),
            pltpu.VMEM((8, dim), F32),
            pltpu.VMEM((n_seq, 1, rows), jnp.int32),
            dma((2 * n_kv // HEAD + 4,)), dma((7,)), dma((4, 3, 3)), dma((4, 3, 3)), dma((4, 3, 3)), dma((4, 3, 3)),
            dma((4,)), dma((4,)), dma((4,)), dma((4,)), dma((n_seq + 1,)), dma((n_seq + 1,)),
        ],
        compiler_params=pltpu.CompilerParams(collective_id=2, has_side_effects=True, vmem_limit_bytes=60 * 2 ** 20),
        cost_estimate=pl.CostEstimate(flops=2 * tokens * dim * (2 * dim + 2 * n_kv), bytes_accessed=40 * 2 ** 20,
                                      transcendentals=0),
    )(x, dy, wq, wk, wv, wo, gain, pos.reshape(tokens, 1), pos[:, None, :], freq)


def solution(mesh):
    cp_size = mesh.shape['cp']

    def shard_fn(hidden, tok_pos, grad_out, norm_gain, w_query, w_key, w_value, w_out):
        n_seq, rows, dim = hidden.shape
        tokens = n_seq * rows
        n_q = w_query.shape[1]
        n_kv = w_key.shape[1]
        groups = n_kv // HEAD
        x16 = hidden.reshape(tokens, dim)
        dy = grad_out.reshape(tokens, dim)
        q, do, r, kv, kv_oth, w_in, w_o, cos2, sin2, gain, pos_oth = gather_project(
            x16, dy, w_query, w_key, w_value, w_out, norm_gain, tok_pos)
        w_in = w_in.reshape(dim, n_q + 2 * n_kv)
        w_o = w_o.reshape(n_q, dim)
        o, dq, dkv = attention(q, do, kv.reshape(tokens, -1), kv_oth.reshape(tokens, -1), tok_pos, pos_oth, cos2, sin2)
        x = x16.astype(F32)
        inv = lax.rsqrt(jnp.mean(x * x, axis=1, keepdims=True) + EPS)
        result = (x + dot(o, w_o)).astype(BF16)
        dkv = jnp.transpose(dkv, (0, 2, 1, 3, 4)).reshape(tokens, 2 * n_kv)
        d_in = jnp.concatenate([dq, dkv], axis=1)
        dr = dot(d_in, w_in, NT)
        xh = x * inv
        gp = jnp.sum(dr * xh, axis=0, keepdims=True)
        a = dr * gain
        gx = inv * (a - xh * jnp.mean(a * xh, axis=1, keepdims=True))
        grad_hidden = (dy.astype(F32) + gx).astype(BF16)
        g_in, g_wo, gg = wgrad(o, dy, r, dq, dkv, gp)
        shard = lax.axis_index('fsdp') * cp_size + lax.axis_index('cp')
        g_gain = lax.dynamic_slice(gg[0], (shard * norm_gain.shape[0],), norm_gain.shape)
        g_kv = g_in[:, n_q:].reshape(-1, groups, 2, HEAD)
        return (result.reshape(hidden.shape), grad_hidden.reshape(hidden.shape), g_in[:, :n_q],
                g_kv[:, :, 0].reshape(-1, n_kv), g_kv[:, :, 1].reshape(-1, n_kv), g_wo, g_gain)

    row = P('fsdp', 'cp', None)
    pos = P('fsdp', 'cp')
    w = P(AXES, None)
    g = P(AXES)
    return jax.shard_map(shard_fn, mesh=mesh, in_specs=(row, pos, row, g, w, w, w, w),
                         out_specs=(row, row, w, w, w, w, g), check_vma=False)
```

profile of v0, /device:TPU:0, one launch (start us, length us, event | category | flops | bytes accessed | tf_op | source)
XLA Modules:
  0.0 312.8 jit_solution(10271304409824647164)
XLA Ops:
  0.6 0.7 copy.19
  1.3 1.2 copy.20
  2.5 1.3 broadcast_in_dim.16.prow_ref.pk_ref
  3.8 1.2 maximum_bitcast_fusion
  5.1 88.4 %shard_map.135 = (bf16[1536,1536]{1,0:T(8,128)(2,1)}, bf16[1536,1536]{1,0:T(8,128)(2,1)}, bf16[1536,1536]{1,0:T(8,128)(2,1)}, bf16[6,256,512]{2,1,0:T(8,128)(2,1...) custom-call(bf16[1536,1536]{1,0:T(8,128)(2,1)} %bitcast.36, ...), custom_call_target="tpu_custom_call" | custom-call | flops 16911433728 | bytes 41943040 | tf_op jit(solution)/shard_map/pallas_call | solution.py:554
  93.5 78.9 %shard_map.136 = (bf16[1536,1536]{1,0:T(8,128)(2,1)}, bf16[1536,1536]{1,0:T(8,128)(2,1)}, bf16[12,256,256]{2,1,0:T(8,128)(2,1)}) custom-call(bf16[1536,1536]{1,0:T(8,128)(2,1)} %get-tuple-element.24.q_ref, bf16[1536,1536]{1,0:T(8,128)(2,1)} %get-tuple-element.25.do_ref, bf16[1536,512]{1,0:T(8,128)(2,1)} %bitcast.55, bf16[1536,512]{1,0:T(8,128)(2,1)} %bitcast.56, ...), custom_call_target="tpu_custom_call" | custom-call | flops 16911433728 | bytes 25165824 | tf_op jit(solution)/shard_map/pallas_call | solution.py:123
  172.4 2.4 reshape.80
  174.8 1.1 copy.26
  175.9 0.8 reshape.81.dkv_hbm
  176.7 0.0 copy-start
  176.8 3.9 %multiply_reduce_fusion = f32[6,256]{1,0:T(8,128)S(1)} fusion(bf16[6,256,1536]{2,1,0:T(8,128)(2,1)} %param.8), kind=kLoop, calls=%fused_computation.12 | loop fusion | flops 7076352 | bytes 4724736 | tf_op jit(solution)/shard_map/reduce_sum | solution.py:597
  180.6 17.1 %fusion.8 = (f32[1536]{0:T(1024)S(1)}, f32[1536]{0:T(1024)S(1)}, f32[1536,1536]{1,0:T(8,128)}) fusion(f32[1536]{0:T(1024)S(1)} %rsqrt.12, bf16[6,256,1536]{2,1,0:T(8,128)(2,1)} %param.8, f32[1536]{0:T(1024)S(1)} %reduce.1, bf16[1536,2048]{1,0:T(8,128)(2,1)} %bitcast.50, bf16[1536,512]{1,0:T(8,128)(2,1)S(1)} %reshape.81.dkv_hbm, ...), kind=kOutput, calls=%fused_computation.10 | convolution fusion | flops 9692770304 | bytes 26763264 | tf_op jit(solution)/shard_map/dot_general | solution.py:27
  197.7 0.6 broadcast_in_dim.18.gp_ref
  198.3 85.1 %shard_map.137 = (f32[96,2048]{1,0:T(8,128)}, f32[96,1536]{1,0:T(8,128)}, f32[1,1536]{1,0:T(1,128)}) custom-call(bf16[1536,1536]{1,0:T(8,128)(2,1)} %get-tuple-element.31.o_hbm, bf16[1536,1536]{1,0:T(8,128)(2,1)} %bitcast.40, bf16[1536,1536]{1,0:T(8,128)(2,1)} %get-tuple-element.37.r_hbm, bf16[1536,1536]{1,0:T(8,128)(2,1)} %get-tuple-element.33.dq_hbm, ...), custom_call_target="tpu_custom_call" | custom-call | flops 16911433728 | bytes 31457280 | tf_op jit(solution)/shard_map/pallas_call | solution.py:294
  283.4 1.0 slice.13
  284.4 0.1 reshape.84
  284.6 0.6 slice_reduce_fusion
  285.2 0.6 copy.27
  285.8 0.6 copy.28
  286.5 1.9 slice.12
  288.4 1.2 dynamic-slice_bitcast_fusion
  289.6 10.5 %fusion.7 = bf16[1536,1536]{1,0:T(8,128)(2,1)} fusion(f32[1536,1536]{1,0:T(8,128)} %get-tuple-element.45, f32[1536]{0:T(1024)S(1)} %broadcast_multiply_fusion, f32[1536]{0:T(1024)S(1)} %reduce.1, f32[1536]{0:T(1024)S(1)} %rsqrt.12, bf16[6,256,1536]{2,1,0:T(8,128)(2,1)} %param.10, bf16[6,256,1536]{2,1,0:T(8,128)(2,1)} %param.8), kind=kLoop, calls=%fused_computation.9 | loop fusion | flops 21233664 | bytes 23611392 | tf_op jit(solution)/shard_map/convert_element_type | solution.py:606
  300.0 11.9 %fusion.9 = bf16[1536,1536]{1,0:T(8,128)(2,1)} fusion(bf16[1536,1536]{1,0:T(8,128)(2,1)} %bitcast.37, bf16[1536,1536]{1,0:T(8,128)(2,1)} %get-tuple-element.31.o_hbm, bf16[1536,1536]{1,0:T(8,128)(2,1)S(1)} %bitcast.53), kind=kOutput, calls=%fused_computation.11 | convolution fusion | flops 7254835200 | bytes 18874368 | tf_op jit(solution)/shard_map/dot_general | solution.py:27
  312.0 0.8 copy.30
  (15 shorter events, 0.1 us)
Async XLA Ops:
  172.4 4.3 %copy-start.2 = (f32[1,1536]{1,0:T(1,128)S(1)}, f32[1,1536]{1,0:T(1,128)}, u32[]{:S(2)}) copy-start(f32[1,1536]{1,0:T(1,128)} %get-tuple-element.36) | copy-start | bytes 18436
  176.7 21.0 %copy-start = (bf16[1536,512]{1,0:T(8,128)(2,1)}, bf16[1536,512]{1,0:T(8,128)(2,1)S(1)}, u32[]{:S(2)}) copy-start(bf16[1536,512]{1,0:T(8,128)(2,1)S(1)} %reshape.81.dkv_hbm) | copy-start | bytes 4718596
  283.4 16.6 %slice-start = ((s8[4718592]{0:T(1024)(128)(4,1)}), s8[524288]{0:T(1024)(128)(4,1)S(1)}, s32[]{:S(2)}) async-start(s8[4718592]{0:T(1024)(128)(4,1)} %bitcast.51), calls=%async_computation | async-start | bytes 1048576
  289.6 10.5 %slice-start.1 = ((s8[4718592]{0:T(1024)(128)(4,1)}), s8[4194304]{0:T(1024)(128)(4,1)S(1)}, s32[]{:S(2)}) async-start(s8[4718592]{0:T(1024)(128)(4,1)} %bitcast.51), calls=%async_computation.1 | async-start | bytes 8388608
  300.0 11.9 %copy-start.1 = (f32[96,1536]{1,0:T(8,128)S(1)}, f32[96,1536]{1,0:T(8,128)}, u32[]{:S(2)}) copy-start(f32[96,1536]{1,0:T(8,128)} %get-tuple-element.60) | copy-start | bytes 1769476
where the time goes:
time: 313 us
  Pallas kernels  252 us (81%)
  matrix products  29 us (9%)
  other arithmetic  15.6 us (5%)
  local copies, waits for them, and re-layouts  15 us (5%)
    pallas_call x1, Pallas kernels, gather_project(): pl.pallas_call(functools.partial(gather_kernel, (n_seq, rows, dim, n_kv))...  88.4 us
    pallas_call x1, Pallas kernels, wgrad(): pl.pallas_call(functools.partial(wgrad_kernel, (tokens, dim, width, sub))...  85.1 us
    pallas_call x1, Pallas kernels, attention(): pl.pallas_call(functools.partial(attn_kernel, n_seq, rows, groups, gsize)...  78.9 us
    dot_general x2, matrix products, dot(): return lax.dot_general(a, b, dims, preferred_element_type=F32)  29 us
    convert_element_type x1, other arithmetic, shard_fn(): grad_hidden = (dy.astype(F32) + gx).astype(BF16)  10.5 us

commit v1 on v0

--- a/solution.py
+++ b/solution.py
@@ -104,8 +104,9 @@
             tot = own[i] + rcv[i]
             c2 = cos_ref[pl.ds(r0, rows), :]
             s2 = sin_ref[pl.ds(r0, rows), :]
-            dkv_ref[i, :, :HEAD] = unrope(tot[:, :HEAD], c2, s2).astype(BF16)
-            dkv_ref[i, :, HEAD:] = tot[:, HEAD:].astype(BF16)
+            kc = pl.multiple_of((i % groups) * 2 * HEAD, HEAD)
+            dkv_ref[pl.ds(r0, rows), pl.ds(kc, HEAD)] = unrope(tot[:, :HEAD], c2, s2).astype(BF16)
+            dkv_ref[pl.ds(r0, rows), pl.ds(kc + HEAD, HEAD)] = tot[:, HEAD:].astype(BF16)
             return carry
         lax.fori_loop(0, n_steps, fin, 0)
 
@@ -126,9 +127,9 @@
         in_specs=[blk(gcols), blk(gcols), blk(2 * HEAD), blk(2 * HEAD),
                   pl.BlockSpec((rows, 1), lambda i: (i // groups, 0)), row3, row3,
                   full(tokens, HEAD), full(tokens, HEAD)],
-        out_specs=[blk(gcols), blk(gcols), full(steps, rows, 2 * HEAD)],
+        out_specs=[blk(gcols), blk(gcols), full(tokens, groups * 2 * HEAD)],
         out_shape=[jax.ShapeDtypeStruct(q.shape, BF16), jax.ShapeDtypeStruct(q.shape, BF16),
-                   jax.ShapeDtypeStruct((steps, rows, 2 * HEAD), BF16)],
+                   jax.ShapeDtypeStruct((tokens, groups * 2 * HEAD), BF16)],
         scratch_shapes=[
             pltpu.VMEM((rows, 2 * rows), F32),
             pltpu.VMEM((gsize * rows, 2 * rows), BF16),
@@ -145,9 +146,11 @@
         cost_estimate=pl.CostEstimate(flops=2 * 7 * tokens * 2 * rows * gcols * groups,
                                       bytes_accessed=24 * 2 ** 20, transcendentals=0),
     )(q, do, kv_own, kv_oth, pos.reshape(tokens, 1), pos[:, None, :], pos_oth, cos2, sin2)
-    return o, dq, dkv.reshape(n_seq, groups, rows, 2, HEAD)
+    return o, dq, dkv
 
 COLORS = ('xyz', 'yzx', 'zxy')
+SLIM = ('zxy', 'zyx')
+BLOCK = 256
 
 
 def place():
@@ -166,10 +169,10 @@
     pl.semaphore_wait(barrier, 4)
 
 
-def wgrad_kernel(shapes, o_hbm, dy_hbm, r_hbm, dq_hbm, dkv_hbm, gp_ref,
-                 gin_ref, gwo_ref, gg_ref,
-                 lhs, rhs, g, rcv_a, h, rcv1, rcv2, rcv3, gain_rcv,
-                 load_sem, d2d_send, d2d_recv, ici_send, ici_recv, gain_send, gain_recv, credit):
+def wgrad_kernel(shapes, o_hbm, dy_hbm, r_hbm, dq_hbm, dkv_hbm, x_hbm, wo_hbm, wa_hbm, wb_hbm, wkv_hbm, gain_ref,
+                 gin_ref, gwo_ref, gg_ref, res_hbm, gh_hbm,
+                 lhs, rhs, g, rcv_a, h, rcv1, rcv2, rcv3, gain_rcv, wo, wkv, xb, dyb, dqb, dkvb, outb,
+                 load_sem, w_sem, blk_sem, out_sem, d2d_send, d2d_recv, ici_send, ici_recv, gain_send, gain_recv, credit):
     tokens, dim, width, sub = shapes
     bits, peers = place()
     core = bits['c']
@@ -191,6 +194,58 @@
     load_rhs(0).start()
     load_lhs(1).start()
     load_rhs(1).start()
+    hd = dim // 2
+    w_loads = [pltpu.make_async_copy(a, b, w_sem.at[i]) for i, (a, b) in enumerate((
+        (wo_hbm, wo), (wkv_hbm, wkv), (wa_hbm, lhs.at[0, :, pl.ds(0, hd)]), (wb_hbm, lhs.at[0, :, pl.ds(hd, hd)])))]
+    w_loads[0].start()
+    w_loads[1].start()
+    n_blk = tokens // BLOCK
+
+    def blk_loads(b, which):
+        rs = pl.ds(pl.multiple_of(b * BLOCK, BLOCK), BLOCK)
+        srcs = ((x_hbm, xb), (dy_hbm, dyb), (dq_hbm, dqb), (dkv_hbm, dkvb))
+        return [pltpu.make_async_copy(srcs[k][0].at[rs, :], srcs[k][1].at[b % 2], blk_sem.at[k, b % 2])
+                for k in which]
+
+    def out_copy(dst, b):
+        rs = pl.ds(pl.multiple_of(b * BLOCK, BLOCK), BLOCK)
+        return pltpu.make_async_copy(outb.at[b % 2], dst.at[rs, :], out_sem.at[b % 2])
+
+    def blocks(lo, hi, which, dst, body):
+        def run(b, carry):
+            for c in blk_loads(b, which):
+                c.wait()
+
+            @pl.when(b + 1 < n_blk)
+            def _():
+                for c in blk_loads(b + 1, which):
+                    c.start()
+
+            @pl.when(b >= 2)
+            def _():
+                out_copy(dst, b - 2).wait()
+
+            outb[b % 2] = body(b)
+            out_copy(dst, b).start()
+            return carry
+        lax.fori_loop(lo, hi, run, 0)
+
+    def res_body(b):
+        rs = pl.ds(pl.multiple_of(b * BLOCK, BLOCK), BLOCK)
+        return (xb[b % 2].astype(F32) + dot(lhs[0, rs, :], wo[...])).astype(BF16)
+
+    def dr_body(b):
+        xf = xb[b % 2].astype(F32)
+        inv = lax.rsqrt(jnp.mean(xf * xf, axis=1, keepdims=True) + EPS)
+        xh = xf * inv
+        dr = dot(dqb[b % 2], lhs[0], NT) + dot(dkvb[b % 2], wkv[...], NT)
+        gg_ref[...] = gg_ref[...] + jnp.sum(dr * xh, axis=0, keepdims=True)
+        a = dr * gain_ref[...]
+        gx = inv * (a - xh * jnp.mean(a * xh, axis=1, keepdims=True))
+        return (dyb[b % 2].astype(F32) + gx).astype(BF16)
+
+    for c in blk_loads(0, (0,)):
+        c.start()
     meet(peers)
 
     def d2d(t):
@@ -260,29 +315,50 @@
                 k = b1 * 4 + b2 * 2 + b3
                 out[c * sub:(c + 1) * sub, j * width:(j + 1) * width] = h[t, c, k] + rcv3[t, c, 0]
 
-    gg_ref[...] = gp_ref[...]
+    gg_ref[...] = jnp.zeros_like(gg_ref)
 
     def gain_copy(i):
         return pltpu.make_async_remote_copy(gg_ref, gain_rcv.at[i], gain_send.at[i], gain_recv.at[i],
                                             device_id=peers['cxyz'[i]], device_id_type=MESH)
 
-    gain_copy(0).start()
+    def flush(dst):
+        out_copy(dst, n_blk - 2).wait()
+        out_copy(dst, n_blk - 1).wait()
+
+    every = (0, 1, 2, 3)
+    half_blk = n_blk // 3
     for i in range(n + 4):
         if i < n:
             compute(i)
         if 0 <= i - 1 < n:
             fold(i - 1)
-        if i < 4:
-            gain_copy(i).wait()
-            gg_ref[...] = gg_ref[...] + gain_rcv[i]
-            if i < 3:
-                gain_copy(i + 1).start()
         for p in range(3):
             if 0 <= i - 2 - p < n:
                 reduce(i - 2 - p, p)
-
-
-def wgrad(o, dy, r, dq, dkv, gp):
+        if i < 3:
+            if i == 0:
+                w_loads[0].wait()
+            blocks(i * half_blk, (i + 1) * half_blk, (0,), res_hbm, res_body)
+            if i == 2:
+                flush(res_hbm)
+                for c in [*w_loads[2:], *blk_loads(0, every)]:
+                    c.start()
+        elif i < 6:
+            if i == 3:
+                for c in w_loads[1:]:
+                    c.wait()
+            blocks((i - 3) * half_blk, (i - 2) * half_blk, every, gh_hbm, dr_body)
+            if i == 5:
+                flush(gh_hbm)
+                gain_copy(0).start()
+        elif i < 10:
+            gain_copy(i - 6).wait()
+            gg_ref[...] = gg_ref[...] + gain_rcv[i - 6]
+            if i < 9:
+                gain_copy(i - 5).start()
+
+
+def wgrad(o, dy, r, dq, dkv, x, w_o, w_a, w_b, w_kv, gain):
     tokens, dim = o.shape
     width = dkv.shape[1]
     shard = dim // 16
@@ -293,10 +369,10 @@
     dma = pltpu.SemaphoreType.DMA
     return pl.pallas_call(
         functools.partial(wgrad_kernel, (tokens, dim, width, sub)),
-        in_specs=[hbm] * 5 + [vm],
-        out_specs=[vm] * 3,
+        in_specs=[hbm] * 10 + [vm],
+        out_specs=[vm] * 3 + [hbm] * 2,
         out_shape=[jax.ShapeDtypeStruct((shard, dim + width), F32), jax.ShapeDtypeStruct((shard, dim), F32),
-                   jax.ShapeDtypeStruct((1, dim), F32)],
+                   jax.ShapeDtypeStruct((1, dim), F32)] + [jax.ShapeDtypeStruct((tokens, dim), BF16)] * 2,
         scratch_shapes=[
             pltpu.VMEM((2, tokens, dim), BF16),
             pltpu.VMEM((2, tokens, width), BF16),
@@ -307,30 +383,36 @@
             pltpu.VMEM((n, 3, 2, sub, width), F32),
             pltpu.VMEM((n, 3, 1, sub, width), F32),
             pltpu.VMEM((4, 1, dim), F32),
-            dma((2 + n,)), dma((n,)), dma((n,)), dma((n, 3, 3)), dma((n, 3, 3)), dma((4,)), dma((4,)),
+            pltpu.VMEM((dim, dim), BF16),
+            pltpu.VMEM((dim, width), BF16),
+            pltpu.VMEM((2, BLOCK, dim), BF16),
+            pltpu.VMEM((2, BLOCK, dim), BF16),
+            pltpu.VMEM((2, BLOCK, dim), BF16),
+            pltpu.VMEM((2, BLOCK, width), BF16),
+            pltpu.VMEM((2, BLOCK, dim), BF16),
+            dma((2 + n,)), dma((4,)), dma((4, 2)), dma((2,)), dma((n,)), dma((n,)), dma((n, 3, 3)), dma((n, 3, 3)), dma((4,)), dma((4,)),
             pltpu.SemaphoreType.REGULAR,
         ],
         compiler_params=pltpu.CompilerParams(collective_id=1, has_side_effects=True, vmem_limit_bytes=60 * 2 ** 20),
         cost_estimate=pl.CostEstimate(flops=2 * tokens * dim * (2 * dim + width), bytes_accessed=30 * 2 ** 20,
                                       transcendentals=0),
-    )(o, dy, r, dq, dkv, gp)
+    )(o, dy, r, dq, dkv, x, w_o, w_a, w_b, w_kv, gain)
 
 
 def gather_kernel(shapes, x_hbm, dy_hbm, wq_hbm, wk_hbm, wv_hbm, wo_hbm, gain_ref, pcol_ref, prow_ref, freq_ref,
-                  q_hbm, do_hbm, r_hbm, kvo_hbm, kvx_hbm, wi_hbm, wf_hbm, cos_ref, sin_ref, gain_out, px_out,
-                  x, dy, r, q, do, kvo, kvx, wi, wo, gbuf, grow, px,
+                  q_hbm, do_hbm, r_hbm, kvo_hbm, kvx_hbm, wkv_hbm, wa_hbm, wb_hbm, wf_hbm, cos_ref, sin_ref, gain_out, px_out,
+                  x, dy, r, q, do, kvo, kvx, wkv, wa, wb, wo, gbuf, grow, px,
                   load_sem, out_sem, ici_send, ici_recv, fwd_send, fwd_recv, own_send, own_recv,
                   g_send, g_recv, kv_send, kv_recv):
     n_seq, rows, dim, n_kv = shapes
     bits, peers = place()
     by, bx, bc, bz = (bits[a] for a in 'yxcz')
     shard = dim // 16
-    third, mid = shard // 3, shard // 2
-    fast = [(a, slice(i * third, (i + 1) * third)) for i, a in enumerate(COLORS)]
-    slim = [(a, slice(i * mid, (i + 1) * mid)) for i, a in enumerate(('zxy', 'zyx'))]
+    third, mid = shard // 3, shard // len(SLIM)
     hq = dim // 2
-    pieces = [(wi, slice(dim, dim + 2 * n_kv), fast), (wo, slice(0, dim), slim),
-              (wi, slice(0, hq), slim), (wi, slice(hq, dim), slim)]
+    fast = COLORS
+    slim = SLIM
+    pieces = [(wkv, fast), (wo, slim), (wa, slim), (wb, slim)]
 
     loads = []
 
@@ -340,22 +422,28 @@
         loads.append(c)
         return len(loads) - 1
 
-    mine = lambda ref, cols: ref.at[by, bx, bc, bz, :, cols]
-    for g in range(n_kv // HEAD):
-        hc = slice(g * HEAD, (g + 1) * HEAD)
-        load(wk_hbm.at[:, hc], mine(wi, slice(dim + 2 * g * HEAD, dim + (2 * g + 1) * HEAD)))
-        load(wv_hbm.at[:, hc], mine(wi, slice(dim + (2 * g + 1) * HEAD, dim + (2 * g + 2) * HEAD)))
+    mine = lambda ref: ref.at[by, bx, bc, bz]
+    for c in range(3):
+        for g in range(n_kv // HEAD):
+            hc = slice(g * HEAD, (g + 1) * HEAD)
+            rws = slice(c * third, (c + 1) * third)
+            for j, w_hbm in enumerate((wk_hbm, wv_hbm)):
+                oc = slice((2 * g + j) * HEAD, (2 * g + j + 1) * HEAD)
+                load(w_hbm.at[rws, hc], wkv.at[by, bx, bc, bz, c, :, oc])
     n_first = len(loads)
-    l_o = load(wo_hbm, mine(wo, slice(0, dim)))
-    l_q = load(wq_hbm, mine(wi, slice(0, dim)))
+    for c in range(len(SLIM)):
+        rws = slice(c * mid, (c + 1) * mid)
+        load(wo_hbm.at[rws, :], wo.at[by, bx, bc, bz, c])
+        load(wq_hbm.at[rws, slice(0, hq)], wa.at[by, bx, bc, bz, c])
+        load(wq_hbm.at[rws, slice(hq, dim)], wb.at[by, bx, bc, bz, c])
+    n_all = len(loads)
     l_x = load(x_hbm, x)
     l_dy = load(dy_hbm, dy)
     gbuf[by, bx, bc, bz] = gain_ref[...]
     meet(peers)
 
     def region(p, c, f, flip):
-        ref, cols, colors = pieces[p]
-        order, rws = colors[c]
+        ref, order = pieces[p][0], pieces[p][1][c]
         idx = []
         for a in 'yxcz':
             if a in order[:f]:
@@ -364,12 +452,12 @@
                 idx.append(1 - bits[a])
             else:
                 idx.append(bits[a])
-        return ref.at[idx[0], idx[1], idx[2], idx[3], rws, cols]
+        return ref.at[idx[0], idx[1], idx[2], idx[3], c]
 
     def ici(p, c, f):
         s = region(p, c, f, False)
         return pltpu.make_async_remote_copy(s, s, ici_send.at[p, c, f], ici_recv.at[p, c, f],
-                                            device_id=peers[pieces[p][2][c][0][f]], device_id_type=MESH)
+                                            device_id=peers[pieces[p][1][c][f]], device_id_type=MESH)
 
     def fwd(p, c, f):
         s = region(p, c, f, True)
@@ -377,17 +465,17 @@
                                             device_id=peers['c'], device_id_type=MESH)
 
     def own(p):
-        s = mine(pieces[p][0], pieces[p][1])
+        s = mine(pieces[p][0])
         return pltpu.make_async_remote_copy(s, s, own_send.at[p], own_recv.at[p],
                                             device_id=peers['c'], device_id_type=MESH)
 
     def begin(p):
-        for c in range(len(pieces[p][2])):
+        for c in range(len(pieces[p][1])):
             ici(p, c, 0).start()
         own(p).start()
 
     def advance(p, f):
-        for c in range(len(pieces[p][2])):
+        for c in range(len(pieces[p][1])):
             ici(p, c, f).wait()
             if f < 2:
                 ici(p, c, f + 1).start()
@@ -395,7 +483,7 @@
 
     def settle(p):
         own(p).wait()
-        for c in range(len(pieces[p][2])):
+        for c in range(len(pieces[p][1])):
             for f in range(3):
                 fwd(p, c, f).wait()
 
@@ -417,9 +505,9 @@
         loads[i].wait()
     begin(0)
     px_copy().start()
-    loads[l_o].wait()
+    for i in range(n_first, n_all):
+        loads[i].wait()
     begin(1)
-    loads[l_q].wait()
     begin(2)
     begin(3)
     gain_copy(0).wait()
@@ -438,11 +526,14 @@
     gain_copy(1).wait()
     gain_copy(2).start()
     advance(0, 0)
+    advance(1, 0)
     lax.fori_loop(n_seq // 2, n_seq, tables, 0)
     gain_copy(2).wait()
     gain_copy(3).start()
     advance(0, 1)
+    advance(2, 0)
     gain_copy(3).wait()
+    advance(3, 0)
     lane = lax.broadcasted_iota(jnp.int32, (8, HEAD), 1)
     for b in range(dim // HEAD):
         acc = jnp.zeros((8, HEAD), F32)
@@ -468,13 +559,11 @@
     r_out = pltpu.make_async_copy(r, r_hbm, out_sem.at[0])
     r_out.start()
     advance(0, 2)
-    advance(1, 0)
     settle(0)
 
     def kv_proj(i, carry):
         rs = pl.ds(pl.multiple_of(i * rows, rows), rows)
-        w = wi[:, :, :, :, :, dim:dim + 2 * n_kv].reshape(dim, 2 * n_kv)
-        kv = dot(r[rs, :], w)
+        kv = dot(r[rs, :], wkv[...].reshape(dim, 2 * n_kv))
         for g in range(n_kv // HEAD):
             kc = slice(2 * g * HEAD, (2 * g + 1) * HEAD)
             vc = slice((2 * g + 1) * HEAD, (2 * g + 2) * HEAD)
@@ -487,7 +576,8 @@
     kvo_out = pltpu.make_async_copy(kvo, kvo_hbm, out_sem.at[1])
     kvo_out.start()
     advance(1, 1)
-    advance(2, 0)
+    advance(2, 1)
+    advance(3, 1)
     advance(1, 2)
     settle(1)
     loads[l_dy].wait()
@@ -500,7 +590,7 @@
     def q_proj(half):
         def body(i, carry):
             rs = pl.ds(pl.multiple_of(i * rows, rows), rows)
-            res = dot(r[rs, :], wi[:, :, :, :, :, half * hq:(half + 1) * hq].reshape(dim, hq))
+            res = dot(r[rs, :], (wa, wb)[half][...].reshape(dim, hq))
             for h in range(hq // HEAD):
                 hc = slice(h * HEAD, (h + 1) * HEAD)
                 q[rs, half * hq + h * HEAD:half * hq + (h + 1) * HEAD] = rope(
@@ -509,21 +599,20 @@
         return body
 
     lax.fori_loop(0, n_seq // 2, do_proj, 0)
-    advance(2, 1)
-    advance(3, 0)
+    advance(2, 2)
     lax.fori_loop(n_seq // 2, n_seq, do_proj, 0)
+    advance(3, 2)
     do_out = pltpu.make_async_copy(do, do_hbm, out_sem.at[2])
     do_out.start()
     wf_out = pltpu.make_async_copy(wo, wf_hbm, out_sem.at[3])
     wf_out.start()
-    advance(2, 2)
-    advance(3, 1)
     settle(2)
     lax.fori_loop(0, n_seq, q_proj(0), 0)
-    advance(3, 2)
     settle(3)
-    wi_out = pltpu.make_async_copy(wi, wi_hbm, out_sem.at[4])
-    wi_out.start()
+    wi_out = [pltpu.make_async_copy(v, o, out_sem.at[7 + i])
+              for i, (v, o) in enumerate(((wkv, wkv_hbm), (wa, wa_hbm), (wb, wb_hbm)))]
+    for c in wi_out:
+        c.start()
     lax.fori_loop(0, n_seq, q_proj(1), 0)
     q_out = pltpu.make_async_copy(q, q_hbm, out_sem.at[5])
     q_out.start()
@@ -533,7 +622,7 @@
         kv_copy(i).wait()
     kvx_out = pltpu.make_async_copy(kvx, kvx_hbm, out_sem.at[6])
     kvx_out.start()
-    for c in (r_out, kvo_out, do_out, wf_out, wi_out, q_out, kvx_out):
+    for c in (r_out, kvo_out, do_out, wf_out, q_out, kvx_out, *wi_out):
         c.wait()
 
 
@@ -550,25 +639,25 @@
     vm = pl.BlockSpec(memory_space=pltpu.VMEM)
     dma = pltpu.SemaphoreType.DMA
     sds = jax.ShapeDtypeStruct
-    wshape = (2, 2, 2, 2, shard)
+    wshapes = [(2, 2, 2, 2, 3, shard // 3, 2 * n_kv)] + [
+        (2, 2, 2, 2, len(SLIM), shard // len(SLIM), c) for c in (dim // 2, dim // 2, dim)]
     return pl.pallas_call(
         functools.partial(gather_kernel, (n_seq, rows, dim, n_kv)),
         in_specs=[hbm] * 6 + [vm] * 4,
-        out_specs=[hbm] * 7 + [vm] * 4,
+        out_specs=[hbm] * 9 + [vm] * 4,
         out_shape=[sds((tokens, dim), BF16), sds((tokens, dim), BF16), sds((tokens, dim), BF16),
                    sds((n_seq, rows, 2 * n_kv), BF16), sds((n_seq, rows, 2 * n_kv), BF16),
-                   sds(wshape + (dim + 2 * n_kv,), BF16), sds(wshape + (dim,), BF16),
+                   *[sds(w, BF16) for w in wshapes],
                    sds((tokens, HEAD), F32), sds((tokens, HEAD), F32), sds((1, dim), F32),
                    sds((n_seq, 1, rows), jnp.int32)],
         scratch_shapes=[pltpu.VMEM((tokens, dim), BF16)] * 5 + [
             pltpu.VMEM((n_seq, rows, 2 * n_kv), BF16),
             pltpu.VMEM((n_seq, rows, 2 * n_kv), BF16),
-            pltpu.VMEM(wshape + (dim + 2 * n_kv,), BF16),
-            pltpu.VMEM(wshape + (dim,), BF16),
+            *[pltpu.VMEM(w, BF16) for w in wshapes],
             pltpu.VMEM((2, 2, 2, 2, 1, HEAD), F32),
             pltpu.VMEM((8, dim), F32),
             pltpu.VMEM((n_seq, 1, rows), jnp.int32),
-            dma((2 * n_kv // HEAD + 4,)), dma((7,)), dma((4, 3, 3)), dma((4, 3, 3)), dma((4, 3, 3)), dma((4, 3, 3)),
+            dma((6 * n_kv // HEAD + 2 + 3 * len(SLIM),)), dma((10,)), dma((4, 3, 3)), dma((4, 3, 3)), dma((4, 3, 3)), dma((4, 3, 3)),
             dma((4,)), dma((4,)), dma((4,)), dma((4,)), dma((n_seq + 1,)), dma((n_seq + 1,)),
         ],
         compiler_params=pltpu.CompilerParams(collective_id=2, has_side_effects=True, vmem_limit_bytes=60 * 2 ** 20),
@@ -588,23 +677,11 @@
         groups = n_kv // HEAD
         x16 = hidden.reshape(tokens, dim)
         dy = grad_out.reshape(tokens, dim)
-        q, do, r, kv, kv_oth, w_in, w_o, cos2, sin2, gain, pos_oth = gather_project(
+        q, do, r, kv, kv_oth, w_kv, w_a, w_b, w_o, cos2, sin2, gain, pos_oth = gather_project(
             x16, dy, w_query, w_key, w_value, w_out, norm_gain, tok_pos)
-        w_in = w_in.reshape(dim, n_q + 2 * n_kv)
-        w_o = w_o.reshape(n_q, dim)
+        w_a, w_b, w_kv, w_o = (w.reshape(dim, -1) for w in (w_a, w_b, w_kv, w_o))
         o, dq, dkv = attention(q, do, kv.reshape(tokens, -1), kv_oth.reshape(tokens, -1), tok_pos, pos_oth, cos2, sin2)
-        x = x16.astype(F32)
-        inv = lax.rsqrt(jnp.mean(x * x, axis=1, keepdims=True) + EPS)
-        result = (x + dot(o, w_o)).astype(BF16)
-        dkv = jnp.transpose(dkv, (0, 2, 1, 3, 4)).reshape(tokens, 2 * n_kv)
-        d_in = jnp.concatenate([dq, dkv], axis=1)
-        dr = dot(d_in, w_in, NT)
-        xh = x * inv
-        gp = jnp.sum(dr * xh, axis=0, keepdims=True)
-        a = dr * gain
-        gx = inv * (a - xh * jnp.mean(a * xh, axis=1, keepdims=True))
-        grad_hidden = (dy.astype(F32) + gx).astype(BF16)
-        g_in, g_wo, gg = wgrad(o, dy, r, dq, dkv, gp)
+        g_in, g_wo, gg, result, grad_hidden = wgrad(o, dy, r, dq, dkv, x16, w_o, w_a, w_b, w_kv, gain)
         shard = lax.axis_index('fsdp') * cp_size + lax.axis_index('cp')
         g_gain = lax.dynamic_slice(gg[0], (shard * norm_gain.shape[0],), norm_gain.shape)
         g_kv = g_in[:, n_q:].reshape(-1, groups, 2, HEAD)

time: 313 us -> 270 us (0.86)
  matrix products: 29 us -> 0 us
  other arithmetic: 15.6 us -> 1.26 us
    dot_general x2 -> x0, matrix products: 29 us -> none  [dot(): return lax.dot_general(a, b, dims, preferred_element_type=F32)]
    convert_element_type x1 -> x0, other arithmetic: 10.5 us -> none  [shard_fn(): grad_hidden = (dy.astype(F32) + gx).astype(BF16)]
    unnamed x15 -> x13, local copies, waits for them, and re-layouts: 4.02 us -> 11.4 us
    pallas_call x1, Pallas kernels: 88.4 us -> 83 us  [gather_project(): pl.pallas_call(functools.partial(gather_kernel, (n_seq, rows, dim, n_kv))...]
    reshape x3 -> x0, local copies, waits for them, and re-layouts: 4.27 us -> none  [the longest x2 3.44 us: attention(): return (o, dq, dkv.reshape(n_seq, groups, rows, 2, HEAD))]
    reduce_sum x1 -> x0, other arithmetic: 3.86 us -> none  [shard_fn(): inv = lax.rsqrt(jnp.mean(x * x, axis=1, keepdims=True) + EPS)]
    pallas_call x1, Pallas kernels: 85.1 us -> 88.8 us  [wgrad(): pl.pallas_call(functools.partial(wgrad_kernel, (tokens, dim, width, sub))...]
where the time goes in v1:
time: 270 us
  Pallas kernels  250 us (93%)
  local copies, waits for them, and re-layouts  17.6 us (7%)
    pallas_call x1, Pallas kernels, wgrad(): pl.pallas_call(functools.partial(wgrad_kernel, (tokens, dim, width, sub))...  88.8 us
    pallas_call x1, Pallas kernels, gather_project(): pl.pallas_call(functools.partial(gather_kernel, (n_seq, rows, dim, n_kv))...  83 us
    pallas_call x1, Pallas kernels, attention(): pl.pallas_call(functools.partial(attn_kernel, n_seq, rows, groups, gsize)...  78.4 us
    unnamed x13, local copies, waits for them, and re-layouts  11.4 us

profile of v1, /device:TPU:0, one launch (start us, length us, event | category | flops | bytes accessed | tf_op | source)
XLA Modules:
  0.0 269.7 jit_solution(12421350312386535430)
XLA Ops:
  0.6 0.7 copy.17
  1.3 1.2 copy.18
  2.5 1.3 broadcast_in_dim.11.prow_ref.pk_ref
  3.8 1.2 maximum_bitcast_fusion
  5.1 83.0 %shard_map.135 = (bf16[1536,1536]{1,0:T(8,128)(2,1)}, bf16[1536,1536]{1,0:T(8,128)(2,1)}, bf16[1536,1536]{1,0:T(8,128)(2,1)}, bf16[6,256,512]{2,1,0:T(8,128)(2,1...) custom-call(bf16[1536,1536]{1,0:T(8,128)(2,1)} %bitcast.40, ...), custom_call_target="tpu_custom_call" | custom-call | flops 16911433728 | bytes 41943040 | tf_op jit(solution)/shard_map/pallas_call | solution.py:644
  88.0 78.4 %shard_map.136 = (bf16[1536,1536]{1,0:T(8,128)(2,1)}, bf16[1536,1536]{1,0:T(8,128)(2,1)}, bf16[1536,512]{1,0:T(8,128)(2,1)}) custom-call(bf16[1536,1536]{1,0:T(8,128)(2,1)} %get-tuple-element.28.q_ref, bf16[1536,1536]{1,0:T(8,128)(2,1)} %get-tuple-element.29.do_ref, bf16[1536,512]{1,0:T(8,128)(2,1)} %bitcast.48, bf16[1536,512]{1,0:T(8,128)(2,1)} %bitcast.49, ...), custom_call_target="tpu_custom_call" | custom-call | flops 16911433728 | bytes 25165824 | tf_op jit(solution)/shard_map/pallas_call | solution.py:124
  166.4 88.8 %shard_map.137 = (f32[96,2048]{1,0:T(8,128)}, f32[96,1536]{1,0:T(8,128)}, f32[1,1536]{1,0:T(1,128)}, bf16[1536,1536]{1,0:T(8,128)(2,1)}, bf16[1536,1536]{1,0:T(8,128)(2,1)}) custom-call(bf16[1536,1536]{1,0:T(8,128)(2,1)} %get-tuple-element.35.o_hbm, bf16[1536,1536]{1,0:T(8,128)(2,1)} %bitcast.43, bf16[1536,1536]{1,0:T(8,128)(2,1)} %get-tuple-element.36.r_hbm, ...), custom_call_target="tpu_custom_call" | custom-call | flops 16911433728 | bytes 31457280 | tf_op jit(solution)/shard_map/pallas_call | solution.py:370
  255.2 0.9 slice.13
  256.2 0.1 reshape.63
  256.3 0.6 slice_reduce_fusion
  256.9 0.6 copy.23
  257.6 0.6 copy.24
  258.2 0.0 slice-start
  258.2 2.0 slice.12
  260.2 1.3 dynamic-slice_bitcast_fusion
  261.4 0.0 slice-start.1
  261.5 5.2 %copy.28 = bf16[6,256,1536]{2,1,0:T(8,128)(2,1)} copy(bf16[6,256,1536]{2,1,0:T(8,128)(2,1)} %bitcast.31) | data formatting | bytes 9437184
  266.7 0.0 slice-done
  266.7 0.0 slice-done.1
  266.7 0.0 copy-start
  266.7 2.2 copy.29
  268.9 0.0 copy-done
  268.9 0.8 copy.30
  (2 shorter events, 0.0 us)
Async XLA Ops:
  258.2 8.5 %slice-start = ((s8[4718592]{0:T(1024)(128)(4,1)}), s8[524288]{0:T(1024)(128)(4,1)S(1)}, s32[]{:S(2)}) async-start(s8[4718592]{0:T(1024)(128)(4,1)} %bitcast.28), calls=%async_computation | async-start | bytes 1048576
  261.4 5.2 %slice-start.1 = ((s8[4718592]{0:T(1024)(128)(4,1)}), s8[4194304]{0:T(1024)(128)(4,1)S(1)}, s32[]{:S(2)}) async-start(s8[4718592]{0:T(1024)(128)(4,1)} %bitcast.28), calls=%async_computation.1 | async-start | bytes 8388608
  266.7 2.2 copy-start

commit v2 on v1

--- a/solution.py
+++ b/solution.py
@@ -3,6 +3,7 @@
 
 import jax
 import jax.numpy as jnp
+import numpy as np
 from jax import lax
 from jax.experimental import pallas as pl
 from jax.experimental.pallas import tpu as pltpu
@@ -27,6 +28,21 @@
     return lax.dot_general(a, b, dims, preferred_element_type=F32)
 
 
+def loop(lo, hi, body):
+    def run(i, carry):
+        body(i)
+        return carry
+    lax.fori_loop(lo, hi, run, None)
+
+
+def span(i, size):
+    return pl.ds(pl.multiple_of(i * size, size), size)
+
+
+def lanes(i):
+    return slice(i * HEAD, (i + 1) * HEAD)
+
+
 def rope(v, cos2, sin2):
     return v * cos2 + pltpu.roll(v, HEAD // 2, 1) * sin2
 
@@ -55,8 +71,10 @@
     @pl.when(grp == 0)
     def _():
         pq = pq_ref[...]
-        mask[:, :rows] = jnp.where(pk_ref[0] <= pq, 0.0, NEG)
-        mask[:, rows:] = jnp.where(px_ref[0] <= pq, 0.0, NEG)
+        for j, ref in enumerate((pk_ref, px_ref)):
+            for b in range(rows // HEAD):
+                key = ref[0, :, lanes(b)].astype(F32)
+                mask[:, lanes(j * (rows // HEAD) + b)] = jnp.where(key <= pq, 0.0, NEG)
 
     row0 = pl.multiple_of(seq * rows, rows)
     cos2 = cos_ref[pl.ds(row0, rows), :]
@@ -64,7 +82,7 @@
     k = jnp.concatenate([kvo_ref[:, :HEAD], kvx_ref[:, :HEAD]], axis=0)
     v = jnp.concatenate([kvo_ref[:, HEAD:], kvx_ref[:, HEAD:]], axis=0)
     for h in range(gsize):
-        cols = slice(h * HEAD, (h + 1) * HEAD)
+        cols = lanes(h)
         hrow = slice(h * rows, (h + 1) * rows)
         q = q_ref[:, cols]
         do = do_ref[:, cols]
@@ -81,8 +99,8 @@
         ds = (p * (dot(do, v, NT) - delta)).astype(BF16)
         ds_s[hrow, :] = ds
         dq_ref[:, cols] = unrope(dot(ds, k) * SCALE, cos2, sin2).astype(BF16)
-    do6 = jnp.concatenate([do_ref[:, h * HEAD:(h + 1) * HEAD] for h in range(gsize)], axis=0)
-    q6 = jnp.concatenate([q_ref[:, h * HEAD:(h + 1) * HEAD] for h in range(gsize)], axis=0)
+    do6 = jnp.concatenate([do_ref[:, lanes(h)] for h in range(gsize)], axis=0)
+    q6 = jnp.concatenate([q_ref[:, lanes(h)] for h in range(gsize)], axis=0)
     dv = dot(p_s[...], do6, TN)
     dk = dot(ds_s[...], q6, TN) * SCALE
     own[step, :, :HEAD] = dk[:rows]
@@ -111,8 +129,8 @@
         lax.fori_loop(0, n_steps, fin, 0)
 
 
-def attention(q, do, kv_own, kv_oth, pos, pos_oth, cos2, sin2):
-    n_seq, rows = pos.shape
+def attention(q, do, kv_own, kv_oth, pos_col, pos, pos_oth, cos2, sin2):
+    n_seq, _, rows = pos.shape
     groups = kv_own.shape[1] // (2 * HEAD)
     gsize = q.shape[1] // HEAD // groups
     steps = n_seq * groups
@@ -125,7 +143,7 @@
         functools.partial(attn_kernel, n_seq, rows, groups, gsize),
         grid=(steps,),
         in_specs=[blk(gcols), blk(gcols), blk(2 * HEAD), blk(2 * HEAD),
-                  pl.BlockSpec((rows, 1), lambda i: (i // groups, 0)), row3, row3,
+                  pl.BlockSpec((rows, HEAD), lambda i: (i // groups, 0)), row3, row3,
                   full(tokens, HEAD), full(tokens, HEAD)],
         out_specs=[blk(gcols), blk(gcols), full(tokens, groups * 2 * HEAD)],
         out_shape=[jax.ShapeDtypeStruct(q.shape, BF16), jax.ShapeDtypeStruct(q.shape, BF16),
@@ -145,7 +163,7 @@
             vmem_limit_bytes=60 * 2 ** 20),
         cost_estimate=pl.CostEstimate(flops=2 * 7 * tokens * 2 * rows * gcols * groups,
                                       bytes_accessed=24 * 2 ** 20, transcendentals=0),
-    )(q, do, kv_own, kv_oth, pos.reshape(tokens, 1), pos[:, None, :], pos_oth, cos2, sin2)
+    )(q, do, kv_own, kv_oth, pos_col, pos, pos_oth, cos2, sin2)
     return o, dq, dkv
 
 COLORS = ('xyz', 'yzx', 'zxy')
@@ -169,17 +187,25 @@
     pl.semaphore_wait(barrier, 4)
 
 
+def chunk_list(dim, width):
+    half = width // 2
+    out = [('o', 0, half), ('o', half, half)]
+    out += [('o', c, width) for c in range(width, dim, width)]
+    out += [('q', c, width) for c in range(0, dim, width)]
+    return out + [('kv', 0, half), ('kv', half, half)]
+
+
 def wgrad_kernel(shapes, o_hbm, dy_hbm, r_hbm, dq_hbm, dkv_hbm, x_hbm, wo_hbm, wa_hbm, wb_hbm, wkv_hbm, gain_ref,
-                 gin_ref, gwo_ref, gg_ref, res_hbm, gh_hbm,
-                 lhs, rhs, g, rcv_a, h, rcv1, rcv2, rcv3, gain_rcv, wo, wkv, xb, dyb, dqb, dkvb, outb,
-                 load_sem, w_sem, blk_sem, out_sem, d2d_send, d2d_recv, ici_send, ici_recv, gain_send, gain_recv, credit):
+                 gwq_ref, gwk_ref, gwv_ref, gwo_ref, gg_ref, res_hbm, gh_hbm,
+                 lhs, rhs, g, rcv_a, gain_rcv, wo, wkv, xb, dyb, dqb, dkvb, outb,
+                 load_sem, w_sem, blk_sem, out_sem, *rest):
     tokens, dim, width, sub = shapes
     bits, peers = place()
     core = bits['c']
-    chunks = [(0, dy_hbm, j, gwo_ref, j) for j in range(dim // width)]
-    chunks += [(1, dq_hbm, j, gin_ref, j) for j in range(dim // width)]
-    chunks += [(1, dkv_hbm, 0, gin_ref, dim // width)]
+    chunks = chunk_list(dim, width)
     n = len(chunks)
+    h, rcv = rest[:n], [rest[n + t * 3:n + t * 3 + 3] for t in range(n)]
+    d2d_send, d2d_recv, ici_send, ici_recv, gain_send, gain_recv, credit = rest[4 * n:]
     seg = dim // 4
     half = seg // 2
 
@@ -187,8 +213,9 @@
         return pltpu.make_async_copy((o_hbm, r_hbm)[i], lhs.at[i], load_sem.at[i])
 
     def load_rhs(t):
-        src, j = chunks[t][1], chunks[t][2]
-        return pltpu.make_async_copy(src.at[:, pl.ds(j * width, width)], rhs.at[t % 2], load_sem.at[2 + t])
+        kind, col, w = chunks[t]
+        src = {'o': dy_hbm, 'q': dq_hbm, 'kv': dkv_hbm}[kind]
+        return pltpu.make_async_copy(src.at[:, pl.ds(col, w)], rhs.at[t % 2, :, pl.ds(0, w)], load_sem.at[2 + t])
 
     load_lhs(0).start()
     load_rhs(0).start()
@@ -249,33 +276,33 @@
     meet(peers)
 
     def d2d(t):
-        return pltpu.make_async_remote_copy(g.at[t % 2, :, 1 - core], rcv_a.at[t % 2], d2d_send.at[t], d2d_recv.at[t],
+        w = pl.ds(0, chunks[t][2])
+        return pltpu.make_async_remote_copy(g.at[t % 2, :, 1 - core, :, w], rcv_a.at[t % 2, :, :, w], d2d_send.at[t], d2d_recv.at[t],
                                             device_id=peers['c'], device_id_type=MESH)
 
     def ici(t, c, p):
         b1, b2, b3 = (bits[a] for a in COLORS[c])
         if p == 0:
-            src, dst = h.at[t, c, pl.ds((1 - b1) * 4, 4)], rcv1.at[t, c]
+            src = h[t].at[c, pl.ds((1 - b1) * 4, 4)]
         elif p == 1:
-            src, dst = h.at[t, c, pl.ds(b1 * 4 + (1 - b2) * 2, 2)], rcv2.at[t, c]
+            src = h[t].at[c, pl.ds(b1 * 4 + (1 - b2) * 2, 2)]
         else:
-            src, dst = h.at[t, c, pl.ds(b1 * 4 + b2 * 2 + (1 - b3), 1)], rcv3.at[t, c]
-        return pltpu.make_async_remote_copy(src, dst, ici_send.at[t, c, p], ici_recv.at[t, c, p],
+            src = h[t].at[c, pl.ds(b1 * 4 + b2 * 2 + (1 - b3), 1)]
+        return pltpu.make_async_remote_copy(src, rcv[t][p].at[c], ici_send.at[t, c, p], ici_recv.at[t, c, p],
                                             device_id=peers[COLORS[c][p]], device_id_type=MESH)
 
     def compute(t):
-        li = chunks[t][0]
-        if t == 0 or chunks[t - 1][0] != li:
+        kind, _, w = chunks[t]
+        li = int(kind != 'o')
+        if t == 0 or (li and chunks[t - 1][0] == 'o'):
             load_lhs(li).wait()
         load_rhs(t).wait()
 
-        def body(yx, carry):
-            cols = pl.ds(pl.multiple_of(yx * seg, HEAD), seg)
-            res = dot(lhs[li, :, cols], rhs[t % 2], TN)
-            g[t % 2, yx, 0] = res[:half]
-            g[t % 2, yx, 1] = res[half:]
-            return carry
-        lax.fori_loop(0, 4, body, 0)
+        def body(yx):
+            res = dot(lhs[li, :, span(yx, seg)], rhs[t % 2, :, :w], TN)
+            g[t % 2, yx, 0, :, :w] = res[:half]
+            g[t % 2, yx, 1, :, :w] = res[half:]
+        loop(0, 4, body)
         if t + 2 < n:
             load_rhs(t + 2).start()
         if t >= 2:
@@ -283,6 +310,7 @@
         d2d(t).start()
 
     def fold(t):
+        w = chunks[t][2]
         d2d(t).wait()
         for y in range(2):
             for x in range(2):
@@ -291,7 +319,7 @@
                     for c in range(3):
                         a1, a2, a3 = (at[a] for a in COLORS[c])
                         rows = slice(z * 3 * sub + c * sub, z * 3 * sub + (c + 1) * sub)
-                        h[t, c, a1 * 4 + a2 * 2 + a3] = g[t % 2, y * 2 + x, core, rows] + rcv_a[t % 2, y * 2 + x, rows]
+                        h[t][c, a1 * 4 + a2 * 2 + a3] = g[t % 2, y * 2 + x, core, rows, :w] + rcv_a[t % 2, y * 2 + x, rows, :w]
         for c in range(3):
             ici(t, c, 0).start()
         if t + 2 < n:
@@ -301,19 +329,21 @@
         for c in range(3):
             b1, b2, b3 = (bits[a] for a in COLORS[c])
             ici(t, c, p).wait()
-            if p == 0:
-                for j in range(4):
-                    h[t, c, b1 * 4 + j] = h[t, c, b1 * 4 + j] + rcv1[t, c, j]
-                ici(t, c, 1).start()
-            elif p == 1:
-                for j in range(2):
-                    k = b1 * 4 + b2 * 2 + j
-                    h[t, c, k] = h[t, c, k] + rcv2[t, c, j]
-                ici(t, c, 2).start()
+            k = (0, b1 * 4, b1 * 4 + b2 * 2, b1 * 4 + b2 * 2 + b3)[p + 1]
+            if p < 2:
+                for j in range(4 >> p):
+                    h[t][c, k + j] = h[t][c, k + j] + rcv[t][p][c, j]
+                ici(t, c, p + 1).start()
+                continue
+            kind, col, w = chunks[t]
+            rws = slice(c * sub, (c + 1) * sub)
+            tot = h[t][c, k] + rcv[t][p][c, 0]
+            if kind == 'kv':
+                for j in range(w // HEAD):
+                    b = col // HEAD + j
+                    (gwk_ref, gwv_ref)[b % 2][rws, lanes(b // 2)] = tot[:, lanes(j)]
             else:
-                out, j = chunks[t][3], chunks[t][4]
-                k = b1 * 4 + b2 * 2 + b3
-                out[c * sub:(c + 1) * sub, j * width:(j + 1) * width] = h[t, c, k] + rcv3[t, c, 0]
+                (gwo_ref if kind == 'o' else gwq_ref)[rws, col:col + w] = tot
 
     gg_ref[...] = jnp.zeros_like(gg_ref)
 
@@ -326,7 +356,8 @@
         out_copy(dst, n_blk - 1).wait()
 
     every = (0, 1, 2, 3)
-    half_blk = n_blk // 3
+    third, fill = n_blk // 3, n_blk // 2
+    assert [c[0] for c in chunks].count('o') == 4
     for i in range(n + 4):
         if i < n:
             compute(i)
@@ -335,27 +366,27 @@
         for p in range(3):
             if 0 <= i - 2 - p < n:
                 reduce(i - 2 - p, p)
-        if i < 3:
-            if i == 0:
+        if 2 <= i < 4:
+            if i == 2:
                 w_loads[0].wait()
-            blocks(i * half_blk, (i + 1) * half_blk, (0,), res_hbm, res_body)
-            if i == 2:
+            blocks((i - 2) * fill, (i - 1) * fill, (0,), res_hbm, res_body)
+            if i == 3:
                 flush(res_hbm)
                 for c in [*w_loads[2:], *blk_loads(0, every)]:
                     c.start()
-        elif i < 6:
-            if i == 3:
+        elif 4 <= i < 7:
+            if i == 4:
                 for c in w_loads[1:]:
                     c.wait()
-            blocks((i - 3) * half_blk, (i - 2) * half_blk, every, gh_hbm, dr_body)
-            if i == 5:
+            blocks((i - 4) * third, (i - 3) * third, every, gh_hbm, dr_body)
+            if i == 6:
                 flush(gh_hbm)
                 gain_copy(0).start()
-        elif i < 10:
-            gain_copy(i - 6).wait()
-            gg_ref[...] = gg_ref[...] + gain_rcv[i - 6]
-            if i < 9:
-                gain_copy(i - 5).start()
+        elif 7 <= i < 11:
+            gain_copy(i - 7).wait()
+            gg_ref[...] = gg_ref[...] + gain_rcv[i - 7]
+            if i < 10:
+                gain_copy(i - 6).start()
 
 
 def wgrad(o, dy, r, dq, dkv, x, w_o, w_a, w_b, w_kv, gain):
@@ -363,34 +394,30 @@
     width = dkv.shape[1]
     shard = dim // 16
     sub = shard // 3
-    n = 2 * (dim // width) + 1
+    chunks = chunk_list(dim, width)
+    n = len(chunks)
     hbm = pl.BlockSpec(memory_space=pl.ANY)
     vm = pl.BlockSpec(memory_space=pltpu.VMEM)
     dma = pltpu.SemaphoreType.DMA
     return pl.pallas_call(
         functools.partial(wgrad_kernel, (tokens, dim, width, sub)),
         in_specs=[hbm] * 10 + [vm],
-        out_specs=[vm] * 3 + [hbm] * 2,
-        out_shape=[jax.ShapeDtypeStruct((shard, dim + width), F32), jax.ShapeDtypeStruct((shard, dim), F32),
-                   jax.ShapeDtypeStruct((1, dim), F32)] + [jax.ShapeDtypeStruct((tokens, dim), BF16)] * 2,
+        out_specs=[vm] * 5 + [hbm] * 2,
+        out_shape=[jax.ShapeDtypeStruct(a, F32) for a in (
+            (shard, dim), (shard, width // 2), (shard, width // 2), (shard, dim), (1, dim))] + [jax.ShapeDtypeStruct((tokens, dim), BF16)] * 2,
         scratch_shapes=[
             pltpu.VMEM((2, tokens, dim), BF16),
             pltpu.VMEM((2, tokens, width), BF16),
             pltpu.VMEM((2, 4, 2, dim // 8, width), F32),
             pltpu.VMEM((2, 4, dim // 8, width), F32),
-            pltpu.VMEM((n, 3, 8, sub, width), F32),
-            pltpu.VMEM((n, 3, 4, sub, width), F32),
-            pltpu.VMEM((n, 3, 2, sub, width), F32),
-            pltpu.VMEM((n, 3, 1, sub, width), F32),
             pltpu.VMEM((4, 1, dim), F32),
             pltpu.VMEM((dim, dim), BF16),
             pltpu.VMEM((dim, width), BF16),
-            pltpu.VMEM((2, BLOCK, dim), BF16),
-            pltpu.VMEM((2, BLOCK, dim), BF16),
-            pltpu.VMEM((2, BLOCK, dim), BF16),
-            pltpu.VMEM((2, BLOCK, width), BF16),
-            pltpu.VMEM((2, BLOCK, dim), BF16),
-            dma((2 + n,)), dma((4,)), dma((4, 2)), dma((2,)), dma((n,)), dma((n,)), dma((n, 3, 3)), dma((n, 3, 3)), dma((4,)), dma((4,)),
+            *[pltpu.VMEM((2, BLOCK, c), BF16) for c in (dim, dim, dim, width, dim)],
+            dma((2 + n,)), dma((4,)), dma((4, 2)), dma((2,)),
+            *[pltpu.VMEM((3, 8, sub, c[2]), F32) for c in chunks],
+            *[pltpu.VMEM((3, k, sub, c[2]), F32) for c in chunks for k in (4, 2, 1)],
+            *[dma((n,))] * 2, *[dma((n, 3, 3))] * 2, *[dma((4,))] * 2,
             pltpu.SemaphoreType.REGULAR,
         ],
         compiler_params=pltpu.CompilerParams(collective_id=1, has_side_effects=True, vmem_limit_bytes=60 * 2 ** 20),
@@ -399,8 +426,8 @@
     )(o, dy, r, dq, dkv, x, w_o, w_a, w_b, w_kv, gain)
 
 
-def gather_kernel(shapes, x_hbm, dy_hbm, wq_hbm, wk_hbm, wv_hbm, wo_hbm, gain_ref, pcol_ref, prow_ref, freq_ref,
-                  q_hbm, do_hbm, r_hbm, kvo_hbm, kvx_hbm, wkv_hbm, wa_hbm, wb_hbm, wf_hbm, cos_ref, sin_ref, gain_out, px_out,
+def gather_kernel(shapes, x_hbm, dy_hbm, wq_hbm, wk_hbm, wv_hbm, wo_hbm, gain_ref, pos_ref, freq_ref,
+                  q_hbm, do_hbm, r_hbm, kvo_hbm, kvx_hbm, wkv_hbm, wa_hbm, wb_hbm, wf_hbm, cos_ref, sin_ref, gain_out, pcol_out, pos_out, px_out,
                   x, dy, r, q, do, kvo, kvx, wkv, wa, wb, wo, gbuf, grow, px,
                   load_sem, out_sem, ici_send, ici_recv, fwd_send, fwd_recv, own_send, own_recv,
                   g_send, g_recv, kv_send, kv_recv):
@@ -412,7 +439,7 @@
     hq = dim // 2
     fast = COLORS
     slim = SLIM
-    pieces = [(wkv, fast), (wo, slim), (wa, slim), (wb, slim)]
+    pieces = [(wkv, fast), (wo, fast), (wa, slim), (wb, slim)]
 
     loads = []
 
@@ -431,15 +458,17 @@
                 oc = slice((2 * g + j) * HEAD, (2 * g + j + 1) * HEAD)
                 load(w_hbm.at[rws, hc], wkv.at[by, bx, bc, bz, c, :, oc])
     n_first = len(loads)
+    for c in range(3):
+        load(wo_hbm.at[c * third:(c + 1) * third, :], wo.at[by, bx, bc, bz, c])
     for c in range(len(SLIM)):
         rws = slice(c * mid, (c + 1) * mid)
-        load(wo_hbm.at[rws, :], wo.at[by, bx, bc, bz, c])
-        load(wq_hbm.at[rws, slice(0, hq)], wa.at[by, bx, bc, bz, c])
-        load(wq_hbm.at[rws, slice(hq, dim)], wb.at[by, bx, bc, bz, c])
+        load(wq_hbm.at[rws, :hq], wa.at[by, bx, bc, bz, c])
+        load(wq_hbm.at[rws, hq:], wb.at[by, bx, bc, bz, c])
     n_all = len(loads)
     l_x = load(x_hbm, x)
     l_dy = load(dy_hbm, dy)
-    gbuf[by, bx, bc, bz] = gain_ref[...]
+    gbuf[by, bx, bc, bz] = jnp.zeros((1, HEAD), F32)
+    gbuf[by, bx, bc, bz, :, :shard] = gain_ref[...]
     meet(peers)
 
     def region(p, c, f, flip):
@@ -497,7 +526,7 @@
                                             device_id=peers['z'], device_id_type=MESH)
 
     def px_copy():
-        return pltpu.make_async_remote_copy(prow_ref, px, kv_send.at[n_seq], kv_recv.at[n_seq],
+        return pltpu.make_async_remote_copy(pos_ref, px, kv_send.at[n_seq], kv_recv.at[n_seq],
                                             device_id=peers['z'], device_id_type=MESH)
 
     gain_copy(0).start()
@@ -507,33 +536,36 @@
     px_copy().start()
     for i in range(n_first, n_all):
         loads[i].wait()
-    begin(1)
-    begin(2)
-    begin(3)
+    for p in (1, 2, 3):
+        begin(p)
     gain_copy(0).wait()
     gain_copy(1).start()
 
-    def tables(i, carry):
-        rs = pl.ds(pl.multiple_of(i * rows, rows), rows)
-        ang = pcol_ref[rs, :].astype(F32) * freq_ref[...]
+    def tables(i):
+        rs = span(i, rows)
+        row = pos_ref[pl.ds(i, 1), :]
+        pos_out[i] = row
+        col = jnp.transpose(jnp.broadcast_to(row.astype(F32), (HEAD, rows)))
+        pcol_out[rs, :] = col
+        ang = col * freq_ref[...]
         lane = lax.broadcasted_iota(jnp.int32, (rows, HEAD), 1)
         cos_ref[rs, :] = jnp.cos(ang)
         sn = jnp.sin(ang)
         sin_ref[rs, :] = jnp.where(lane < HEAD // 2, -sn, sn)
-        return carry
-
-    lax.fori_loop(0, n_seq // 2, tables, 0)
+
+    mid_seq = n_seq // 2
+    loop(0, mid_seq, tables)
     gain_copy(1).wait()
     gain_copy(2).start()
     advance(0, 0)
     advance(1, 0)
-    lax.fori_loop(n_seq // 2, n_seq, tables, 0)
+    loop(mid_seq, n_seq, tables)
     gain_copy(2).wait()
     gain_copy(3).start()
     advance(0, 1)
+    advance(1, 1)
+    gain_copy(3).wait()
     advance(2, 0)
-    gain_copy(3).wait()
-    advance(3, 0)
     lane = lax.broadcasted_iota(jnp.int32, (8, HEAD), 1)
     for b in range(dim // HEAD):
         acc = jnp.zeros((8, HEAD), F32)
@@ -548,81 +580,80 @@
     gain_out[...] = grow[0:1, :]
     loads[l_x].wait()
 
-    def norm(i, carry):
-        rs = pl.ds(pl.multiple_of(i * rows // 2, rows // 2), rows // 2)
+    def norm(i):
+        rs = span(i, rows // 2)
         xf = x[rs, :].astype(F32)
         inv = lax.rsqrt(jnp.mean(xf * xf, axis=1, keepdims=True) + EPS)
         r[rs, :] = (xf * inv * grow[0:1, :]).astype(BF16)
-        return carry
-
-    lax.fori_loop(0, 2 * n_seq, norm, 0)
+
+    loop(0, 2 * n_seq, norm)
     r_out = pltpu.make_async_copy(r, r_hbm, out_sem.at[0])
     r_out.start()
     advance(0, 2)
+    advance(3, 0)
     settle(0)
-
-    def kv_proj(i, carry):
-        rs = pl.ds(pl.multiple_of(i * rows, rows), rows)
+    wkv_out = pltpu.make_async_copy(wkv, wkv_hbm, out_sem.at[4])
+    wkv_out.start()
+
+    def kv_proj(i):
+        rs = span(i, rows)
         kv = dot(r[rs, :], wkv[...].reshape(dim, 2 * n_kv))
-        for g in range(n_kv // HEAD):
-            kc = slice(2 * g * HEAD, (2 * g + 1) * HEAD)
-            vc = slice((2 * g + 1) * HEAD, (2 * g + 2) * HEAD)
-            kvo[i, :, kc] = rope(kv[:, kc], cos_ref[rs, :], sin_ref[rs, :]).astype(BF16)
-            kvo[i, :, vc] = kv[:, vc].astype(BF16)
+        for g in range(0, 2 * n_kv // HEAD, 2):
+            kvo[i, :, lanes(g)] = rope(kv[:, lanes(g)], cos_ref[rs, :], sin_ref[rs, :]).astype(BF16)
+            kvo[i, :, lanes(g + 1)] = kv[:, lanes(g + 1)].astype(BF16)
         kv_copy(i).start()
-        return carry
-
-    lax.fori_loop(0, n_seq, kv_proj, 0)
+
+    loop(0, mid_seq, kv_proj)
+    advance(1, 2)
+    loop(mid_seq, n_seq, kv_proj)
     kvo_out = pltpu.make_async_copy(kvo, kvo_hbm, out_sem.at[1])
     kvo_out.start()
-    advance(1, 1)
     advance(2, 1)
-    advance(3, 1)
-    advance(1, 2)
     settle(1)
+    wf_out = pltpu.make_async_copy(wo, wf_hbm, out_sem.at[3])
+    wf_out.start()
     loads[l_dy].wait()
 
-    def do_proj(i, carry):
-        rs = pl.ds(pl.multiple_of(i * rows, rows), rows)
+    def do_proj(i):
+        rs = span(i, rows)
         do[rs, :] = dot(dy[rs, :], wo[...].reshape(dim, dim), NT).astype(BF16)
-        return carry
 
     def q_proj(half):
-        def body(i, carry):
-            rs = pl.ds(pl.multiple_of(i * rows, rows), rows)
+        def body(i):
+            rs = span(i, rows)
             res = dot(r[rs, :], (wa, wb)[half][...].reshape(dim, hq))
             for h in range(hq // HEAD):
-                hc = slice(h * HEAD, (h + 1) * HEAD)
-                q[rs, half * hq + h * HEAD:half * hq + (h + 1) * HEAD] = rope(
-                    res[:, hc], cos_ref[rs, :], sin_ref[rs, :]).astype(BF16)
-            return carry
+                q[rs, lanes(half * (hq // HEAD) + h)] = rope(res[:, lanes(h)], cos_ref[rs, :], sin_ref[rs, :]).astype(BF16)
         return body
 
-    lax.fori_loop(0, n_seq // 2, do_proj, 0)
+    def q_out(half):
+        hc = slice(half * hq, (half + 1) * hq)
+        return pltpu.make_async_copy(q.at[:, hc], q_hbm.at[:, hc], out_sem.at[7 + half])
+
+    loop(0, mid_seq, do_proj)
+    advance(3, 1)
     advance(2, 2)
-    lax.fori_loop(n_seq // 2, n_seq, do_proj, 0)
-    advance(3, 2)
+    loop(mid_seq, n_seq, do_proj)
     do_out = pltpu.make_async_copy(do, do_hbm, out_sem.at[2])
     do_out.start()
-    wf_out = pltpu.make_async_copy(wo, wf_hbm, out_sem.at[3])
-    wf_out.start()
     settle(2)
-    lax.fori_loop(0, n_seq, q_proj(0), 0)
+    wa_out = pltpu.make_async_copy(wa, wa_hbm, out_sem.at[5])
+    wa_out.start()
+    loop(0, n_seq, q_proj(0))
+    q_out(0).start()
+    advance(3, 2)
     settle(3)
-    wi_out = [pltpu.make_async_copy(v, o, out_sem.at[7 + i])
-              for i, (v, o) in enumerate(((wkv, wkv_hbm), (wa, wa_hbm), (wb, wb_hbm)))]
-    for c in wi_out:
-        c.start()
-    lax.fori_loop(0, n_seq, q_proj(1), 0)
-    q_out = pltpu.make_async_copy(q, q_hbm, out_sem.at[5])
-    q_out.start()
+    wb_out = pltpu.make_async_copy(wb, wb_hbm, out_sem.at[9])
+    wb_out.start()
+    loop(0, n_seq, q_proj(1))
+    q_out(1).start()
     px_copy().wait()
-    px_out[...] = px[...]
     for i in range(n_seq):
+        px_out[i] = px[i:i + 1, :]
         kv_copy(i).wait()
     kvx_out = pltpu.make_async_copy(kvx, kvx_hbm, out_sem.at[6])
     kvx_out.start()
-    for c in (r_out, kvo_out, do_out, wf_out, q_out, kvx_out, *wi_out):
+    for c in (r_out, kvo_out, do_out, wf_out, wkv_out, wa_out, wb_out, q_out(0), q_out(1), kvx_out):
         c.wait()
 
 
@@ -632,38 +663,35 @@
     n_kv = wk.shape[1]
     shard = dim // 16
     half = HEAD // 2
-    freq = THETA ** (-jnp.arange(half, dtype=F32) / half)
-    freq = jnp.concatenate([freq, freq])[None]
-    gain = jnp.pad(gain, (0, HEAD - shard))[None]
+    freq = np.float32(THETA) ** (-np.arange(half, dtype=np.float32) / half)
+    freq = jnp.asarray(np.tile(freq, 2)[None])
     hbm = pl.BlockSpec(memory_space=pl.ANY)
     vm = pl.BlockSpec(memory_space=pltpu.VMEM)
     dma = pltpu.SemaphoreType.DMA
     sds = jax.ShapeDtypeStruct
-    wshapes = [(2, 2, 2, 2, 3, shard // 3, 2 * n_kv)] + [
-        (2, 2, 2, 2, len(SLIM), shard // len(SLIM), c) for c in (dim // 2, dim // 2, dim)]
+    wshapes = [(2, 2, 2, 2, len(k), shard // len(k), c) for k, c in (
+        (COLORS, 2 * n_kv), (SLIM, dim // 2), (SLIM, dim // 2), (COLORS, dim))]
     return pl.pallas_call(
         functools.partial(gather_kernel, (n_seq, rows, dim, n_kv)),
-        in_specs=[hbm] * 6 + [vm] * 4,
-        out_specs=[hbm] * 9 + [vm] * 4,
-        out_shape=[sds((tokens, dim), BF16), sds((tokens, dim), BF16), sds((tokens, dim), BF16),
-                   sds((n_seq, rows, 2 * n_kv), BF16), sds((n_seq, rows, 2 * n_kv), BF16),
-                   *[sds(w, BF16) for w in wshapes],
-                   sds((tokens, HEAD), F32), sds((tokens, HEAD), F32), sds((1, dim), F32),
-                   sds((n_seq, 1, rows), jnp.int32)],
+        in_specs=[hbm] * 6 + [vm] * 3,
+        out_specs=[hbm] * 9 + [vm] * 6,
+        out_shape=[sds((tokens, dim), BF16)] * 3 + [sds((n_seq, rows, 2 * n_kv), BF16)] * 2 + [
+            sds(w, BF16) for w in wshapes] + [sds((tokens, HEAD), F32)] * 2 + [
+            sds((1, dim), F32), sds((tokens, HEAD), F32)] + [sds((n_seq, 1, rows), jnp.int32)] * 2,
         scratch_shapes=[pltpu.VMEM((tokens, dim), BF16)] * 5 + [
             pltpu.VMEM((n_seq, rows, 2 * n_kv), BF16),
             pltpu.VMEM((n_seq, rows, 2 * n_kv), BF16),
             *[pltpu.VMEM(w, BF16) for w in wshapes],
             pltpu.VMEM((2, 2, 2, 2, 1, HEAD), F32),
             pltpu.VMEM((8, dim), F32),
-            pltpu.VMEM((n_seq, 1, rows), jnp.int32),
-            dma((6 * n_kv // HEAD + 2 + 3 * len(SLIM),)), dma((10,)), dma((4, 3, 3)), dma((4, 3, 3)), dma((4, 3, 3)), dma((4, 3, 3)),
-            dma((4,)), dma((4,)), dma((4,)), dma((4,)), dma((n_seq + 1,)), dma((n_seq + 1,)),
+            pltpu.VMEM((n_seq, rows), jnp.int32),
+            dma((6 * n_kv // HEAD + 5 + 2 * len(SLIM),)), dma((10,)), *[dma((4, 3, 3))] * 4,
+            *[dma((4,))] * 4, *[dma((n_seq + 1,))] * 2,
         ],
         compiler_params=pltpu.CompilerParams(collective_id=2, has_side_effects=True, vmem_limit_bytes=60 * 2 ** 20),
         cost_estimate=pl.CostEstimate(flops=2 * tokens * dim * (2 * dim + 2 * n_kv), bytes_accessed=40 * 2 ** 20,
                                       transcendentals=0),
-    )(x, dy, wq, wk, wv, wo, gain, pos.reshape(tokens, 1), pos[:, None, :], freq)
+    )(x, dy, wq, wk, wv, wo, gain[None], pos, freq)
 
 
 def solution(mesh):
@@ -677,20 +705,18 @@
         groups = n_kv // HEAD
         x16 = hidden.reshape(tokens, dim)
         dy = grad_out.reshape(tokens, dim)
-        q, do, r, kv, kv_oth, w_kv, w_a, w_b, w_o, cos2, sin2, gain, pos_oth = gather_project(
+        q, do, r, kv, kv_oth, w_kv, w_a, w_b, w_o, cos2, sin2, gain, pcol, pos, pos_oth = gather_project(
             x16, dy, w_query, w_key, w_value, w_out, norm_gain, tok_pos)
         w_a, w_b, w_kv, w_o = (w.reshape(dim, -1) for w in (w_a, w_b, w_kv, w_o))
-        o, dq, dkv = attention(q, do, kv.reshape(tokens, -1), kv_oth.reshape(tokens, -1), tok_pos, pos_oth, cos2, sin2)
-        g_in, g_wo, gg, result, grad_hidden = wgrad(o, dy, r, dq, dkv, x16, w_o, w_a, w_b, w_kv, gain)
+        o, dq, dkv = attention(q, do, kv.reshape(tokens, -1), kv_oth.reshape(tokens, -1), pcol, pos, pos_oth, cos2, sin2)
+        g_wq, g_wk, g_wv, g_wo, gg, result, grad_hidden = wgrad(o, dy, r, dq, dkv, x16, w_o, w_a, w_b, w_kv, gain)
         shard = lax.axis_index('fsdp') * cp_size + lax.axis_index('cp')
         g_gain = lax.dynamic_slice(gg[0], (shard * norm_gain.shape[0],), norm_gain.shape)
-        g_kv = g_in[:, n_q:].reshape(-1, groups, 2, HEAD)
-        return (result.reshape(hidden.shape), grad_hidden.reshape(hidden.shape), g_in[:, :n_q],
-                g_kv[:, :, 0].reshape(-1, n_kv), g_kv[:, :, 1].reshape(-1, n_kv), g_wo, g_gain)
+        return result.reshape(hidden.shape), grad_hidden.reshape(hidden.shape), g_wq, g_wk, g_wv, g_wo, g_gain
 
     row = P('fsdp', 'cp', None)
-    pos = P('fsdp', 'cp')
+    pos_spec = P('fsdp', 'cp')
     w = P(AXES, None)
     g = P(AXES)
-    return jax.shard_map(shard_fn, mesh=mesh, in_specs=(row, pos, row, g, w, w, w, w),
+    return jax.shard_map(shard_fn, mesh=mesh, in_specs=(row, pos_spec, row, g, w, w, w, w),
                          out_specs=(row, row, w, w, w, w, g), check_vma=False)

time: 270 us -> 251 us (0.930)
  Pallas kernels: 250 us -> 238 us
  local copies, waits for them, and re-layouts: 17.6 us -> 11.6 us
    pallas_call x1, Pallas kernels: 83 us -> 70.6 us  [gather_project(): pl.pallas_call(functools.partial(gather_kernel, (n_seq, rows, dim, n_kv))...]
    slice x3 -> x0, local copies, waits for them, and re-layouts: 3.51 us -> none  [the longest x1 1.97 us: shard_fn(): g_in[:, :n_q]]
    unnamed x13 -> x16, local copies, waits for them, and re-layouts: 11.4 us -> 10.3 us
where the time goes in v2:
time: 251 us
  Pallas kernels  238 us (95%)
  local copies, waits for them, and re-layouts  11.6 us (5%)
    pallas_call x1, Pallas kernels, wgrad(): pl.pallas_call(functools.partial(wgrad_kernel, (tokens, dim, width, sub))...  89.1 us
    pallas_call x1, Pallas kernels, attention(): pl.pallas_call(functools.partial(attn_kernel, n_seq, rows, groups, gsize)...  78.5 us
    pallas_call x1, Pallas kernels, gather_project(): pl.pallas_call(functools.partial(gather_kernel, (n_seq, rows, dim, n_kv))...  70.6 us
    unnamed x16, local copies, waits for them, and re-layouts  10.3 us

profile of v2, /device:TPU:0, one launch (start us, length us, event | category | flops | bytes accessed | tf_op | source)
XLA Modules:
  0.0 250.5 jit_solution(16269521888891937899)
XLA Ops:
  0.6 70.6 %shard_map.144 = (bf16[1536,1536]{1,0:T(8,128)(2,1)}, bf16[1536,1536]{1,0:T(8,128)(2,1)}, bf16[1536,1536]{1,0:T(8,128)(2,1)}, bf16[6,256,512]{2,1,0:T(8,128)(2,1...) custom-call(bf16[1536,1536]{1,0:T(8,128)(2,1)} %bitcast.15, ...), custom_call_target="tpu_custom_call" | custom-call | flops 16911433728 | bytes 41943040 | tf_op jit(solution)/shard_map/pallas_call | solution.py:674
  71.3 78.5 %shard_map.145 = (bf16[1536,1536]{1,0:T(8,128)(2,1)}, bf16[1536,1536]{1,0:T(8,128)(2,1)}, bf16[1536,512]{1,0:T(8,128)(2,1)}) custom-call(bf16[1536,1536]{1,0:T(8,128)(2,1)} %get-tuple-element.32.q_ref, bf16[1536,1536]{1,0:T(8,128)(2,1)} %get-tuple-element.33.do_ref, bf16[1536,512]{1,0:T(8,128)(2,1)} %bitcast.24, bf16[1536,512]{1,0:T(8,128)(2,1)} %bitcast.25, ...), custom_call_target="tpu_custom_call" | custom-call | flops 16911433728 | bytes 25165824 | tf_op jit(solution)/shard_map/pallas_call | solution.py:142
  149.8 89.1 %shard_map.146 = (f32[96,1536]{1,0:T(8,128)}, f32[96,256]{1,0:T(8,128)}, f32[96,256]{1,0:T(8,128)}, f32[96,1536]{1,0:T(8,128)}, f32[1,1536]{1,0:T(1,128)}, /*ind...) custom-call(bf16[1536,1536]{1,0:T(8,128)(2,1)} %get-tuple-element.41.o_hbm, bf16[1536,1536]{1,0:T(8,128)(2,1)} %bitcast.18, ...), custom_call_target="tpu_custom_call" | custom-call | flops 16911433728 | bytes 31457280 | tf_op jit(solution)/shard_map/pallas_call | solution.py:402
  238.9 1.3 dynamic-slice_bitcast_fusion
  240.1 0.0 copy-start
  240.1 5.2 %copy.22 = bf16[6,256,1536]{2,1,0:T(8,128)(2,1)} copy(bf16[6,256,1536]{2,1,0:T(8,128)(2,1)} %bitcast.14) | data formatting | bytes 9437184
  245.4 0.0 copy-done
  245.4 0.0 copy-start.2
  245.4 0.0 copy-start.4
  245.4 0.0 copy-start.3
  245.4 0.0 copy-start.1
  245.4 2.2 copy.23
  247.6 0.0 copy-done.2
  247.6 0.8 copy.24
  248.4 0.0 copy-done.4
  248.4 0.6 copy.25
  249.0 0.0 copy-done.3
  249.0 0.6 copy.26
  249.7 0.0 copy-done.1
  249.7 0.8 copy.27
Async XLA Ops:
  240.1 5.2 %copy-start = (bf16[1536,1536]{1,0:T(8,128)(2,1)S(1)}, bf16[1536,1536]{1,0:T(8,128)(2,1)}, u32[]{:S(2)}) copy-start(bf16[1536,1536]{1,0:T(8,128)(2,1)} %get-tuple-element.51) | copy-start | bytes 14155780
  245.4 2.2 copy-start.2
  245.4 3.0 %copy-start.4 = (f32[96,256]{1,0:T(8,128)S(1)}, f32[96,256]{1,0:T(8,128)}, u32[]{:S(2)}) copy-start(f32[96,256]{1,0:T(8,128)} %get-tuple-element.67) | copy-start | bytes 294916
  245.4 3.7 %copy-start.3 = (f32[96,256]{1,0:T(8,128)S(1)}, f32[96,256]{1,0:T(8,128)}, u32[]{:S(2)}) copy-start(f32[96,256]{1,0:T(8,128)} %get-tuple-element.68) | copy-start | bytes 294916
  245.4 4.3 %copy-start.1 = (f32[96,1536]{1,0:T(8,128)S(1)}, f32[96,1536]{1,0:T(8,128)}, u32[]{:S(2)}) copy-start(f32[96,1536]{1,0:T(8,128)} %get-tuple-element.69) | copy-start | bytes 1769476

commit v3 on v2

--- a/solution.py
+++ b/solution.py
@@ -50,121 +50,6 @@
 def unrope(v, cos2, sin2):
     return v * cos2 - pltpu.roll(v, HEAD // 2, 1) * sin2
 
-
-def attn_kernel(n_seq, rows, groups, gsize,
-                q_ref, do_ref, kvo_ref, kvx_ref, pq_ref, pk_ref, px_ref, cos_ref, sin_ref,
-                o_ref, dq_ref, dkv_ref,
-                mask, p_s, ds_s, own, snd, rcv, send_sem, recv_sem):
-    step = pl.program_id(0)
-    n_steps = n_seq * groups
-    seq = step // groups
-    grp = step % groups
-    cp = lax.axis_index('cp')
-    peer = {'cp': 1 - cp}
-
-    @pl.when(step == 0)
-    def _():
-        barrier = pltpu.get_barrier_semaphore()
-        pl.semaphore_signal(barrier, inc=1, device_id=peer, device_id_type=MESH)
-        pl.semaphore_wait(barrier, 1)
-
-    @pl.when(grp == 0)
-    def _():
-        pq = pq_ref[...]
-        for j, ref in enumerate((pk_ref, px_ref)):
-            for b in range(rows // HEAD):
-                key = ref[0, :, lanes(b)].astype(F32)
-                mask[:, lanes(j * (rows // HEAD) + b)] = jnp.where(key <= pq, 0.0, NEG)
-
-    row0 = pl.multiple_of(seq * rows, rows)
-    cos2 = cos_ref[pl.ds(row0, rows), :]
-    sin2 = sin_ref[pl.ds(row0, rows), :]
-    k = jnp.concatenate([kvo_ref[:, :HEAD], kvx_ref[:, :HEAD]], axis=0)
-    v = jnp.concatenate([kvo_ref[:, HEAD:], kvx_ref[:, HEAD:]], axis=0)
-    for h in range(gsize):
-        cols = lanes(h)
-        hrow = slice(h * rows, (h + 1) * rows)
-        q = q_ref[:, cols]
-        do = do_ref[:, cols]
-        s = dot(q, k, NT) * (SCALE * LOG2E) + mask[...]
-        m = jnp.max(s, axis=1, keepdims=True)
-        e = jnp.exp2(s - m)
-        l = jnp.sum(e, axis=1, keepdims=True)
-        rl = 1.0 / l
-        o = (dot(e.astype(BF16), v) * rl).astype(BF16)
-        o_ref[:, cols] = o
-        delta = jnp.sum(do.astype(F32) * o.astype(F32), axis=1, keepdims=True)
-        p = e * rl
-        p_s[hrow, :] = p.astype(BF16)
-        ds = (p * (dot(do, v, NT) - delta)).astype(BF16)
-        ds_s[hrow, :] = ds
-        dq_ref[:, cols] = unrope(dot(ds, k) * SCALE, cos2, sin2).astype(BF16)
-    do6 = jnp.concatenate([do_ref[:, lanes(h)] for h in range(gsize)], axis=0)
-    q6 = jnp.concatenate([q_ref[:, lanes(h)] for h in range(gsize)], axis=0)
-    dv = dot(p_s[...], do6, TN)
-    dk = dot(ds_s[...], q6, TN) * SCALE
-    own[step, :, :HEAD] = dk[:rows]
-    own[step, :, HEAD:] = dv[:rows]
-    snd[step, :, :HEAD] = dk[rows:]
-    snd[step, :, HEAD:] = dv[rows:]
-
-    def copy(i):
-        return pltpu.make_async_remote_copy(snd.at[i], rcv.at[i], send_sem.at[i], recv_sem.at[i],
-                                            device_id=peer, device_id_type=MESH)
-
-    copy(step).start()
-
-    @pl.when(step == n_steps - 1)
-    def _():
-        def fin(i, carry):
-            copy(i).wait()
-            r0 = pl.multiple_of((i // groups) * rows, rows)
-            tot = own[i] + rcv[i]
-            c2 = cos_ref[pl.ds(r0, rows), :]
-            s2 = sin_ref[pl.ds(r0, rows), :]
-            kc = pl.multiple_of((i % groups) * 2 * HEAD, HEAD)
-            dkv_ref[pl.ds(r0, rows), pl.ds(kc, HEAD)] = unrope(tot[:, :HEAD], c2, s2).astype(BF16)
-            dkv_ref[pl.ds(r0, rows), pl.ds(kc + HEAD, HEAD)] = tot[:, HEAD:].astype(BF16)
-            return carry
-        lax.fori_loop(0, n_steps, fin, 0)
-
-
-def attention(q, do, kv_own, kv_oth, pos_col, pos, pos_oth, cos2, sin2):
-    n_seq, _, rows = pos.shape
-    groups = kv_own.shape[1] // (2 * HEAD)
-    gsize = q.shape[1] // HEAD // groups
-    steps = n_seq * groups
-    gcols = gsize * HEAD
-    tokens = n_seq * rows
-    blk = lambda c: pl.BlockSpec((rows, c), lambda i: (i // groups, i % groups))
-    row3 = pl.BlockSpec((1, 1, rows), lambda i: (i // groups, 0, 0))
-    full = lambda *s: pl.BlockSpec(s, lambda i: (0,) * len(s))
-    o, dq, dkv = pl.pallas_call(
-        functools.partial(attn_kernel, n_seq, rows, groups, gsize),
-        grid=(steps,),
-        in_specs=[blk(gcols), blk(gcols), blk(2 * HEAD), blk(2 * HEAD),
-                  pl.BlockSpec((rows, HEAD), lambda i: (i // groups, 0)), row3, row3,
-                  full(tokens, HEAD), full(tokens, HEAD)],
-        out_specs=[blk(gcols), blk(gcols), full(tokens, groups * 2 * HEAD)],
-        out_shape=[jax.ShapeDtypeStruct(q.shape, BF16), jax.ShapeDtypeStruct(q.shape, BF16),
-                   jax.ShapeDtypeStruct((tokens, groups * 2 * HEAD), BF16)],
-        scratch_shapes=[
-            pltpu.VMEM((rows, 2 * rows), F32),
-            pltpu.VMEM((gsize * rows, 2 * rows), BF16),
-            pltpu.VMEM((gsize * rows, 2 * rows), BF16),
-            pltpu.VMEM((steps, rows, 2 * HEAD), F32),
-            pltpu.VMEM((steps, rows, 2 * HEAD), F32),
-            pltpu.VMEM((steps, rows, 2 * HEAD), F32),
-            pltpu.SemaphoreType.DMA((steps,)),
-            pltpu.SemaphoreType.DMA((steps,)),
-        ],
-        compiler_params=pltpu.CompilerParams(
-            collective_id=0, has_side_effects=True, dimension_semantics=('arbitrary',),
-            vmem_limit_bytes=60 * 2 ** 20),
-        cost_estimate=pl.CostEstimate(flops=2 * 7 * tokens * 2 * rows * gcols * groups,
-                                      bytes_accessed=24 * 2 ** 20, transcendentals=0),
-    )(q, do, kv_own, kv_oth, pos_col, pos, pos_oth, cos2, sin2)
-    return o, dq, dkv
 
 COLORS = ('xyz', 'yzx', 'zxy')
 SLIM = ('zxy', 'zyx')
@@ -427,16 +312,19 @@
 
 
 def gather_kernel(shapes, x_hbm, dy_hbm, wq_hbm, wk_hbm, wv_hbm, wo_hbm, gain_ref, pos_ref, freq_ref,
-                  q_hbm, do_hbm, r_hbm, kvo_hbm, kvx_hbm, wkv_hbm, wa_hbm, wb_hbm, wf_hbm, cos_ref, sin_ref, gain_out, pcol_out, pos_out, px_out,
-                  x, dy, r, q, do, kvo, kvx, wkv, wa, wb, wo, gbuf, grow, px,
-                  load_sem, out_sem, ici_send, ici_recv, fwd_send, fwd_recv, own_send, own_recv,
-                  g_send, g_recv, kv_send, kv_recv):
+                  r_hbm, o_hbm, dq_hbm, wkv_hbm, wa_hbm, wb_hbm, wf_hbm, gain_out, dkv_out,
+                  x, dy, r, q, do, kvo, kvx, wkv, wa, wb, wo, gbuf, grow, px, cos_ref, sin_ref, pcol,
+                  mask, p_s, ds_s, mine_kv, snd, rcv,
+                  load_sem, out_sem, blk_sem, ici_send, ici_recv, fwd_send, fwd_recv, own_send, own_recv,
+                  g_send, g_recv, kv_send, kv_recv, dkv_send, dkv_recv):
     n_seq, rows, dim, n_kv = shapes
     bits, peers = place()
     by, bx, bc, bz = (bits[a] for a in 'yxcz')
     shard = dim // 16
     third, mid = shard // 3, shard // len(SLIM)
     hq = dim // 2
+    groups = n_kv // HEAD
+    gsize = dim // HEAD // groups
     fast = COLORS
     slim = SLIM
     pieces = [(wkv, fast), (wo, fast), (wa, slim), (wb, slim)]
@@ -544,9 +432,8 @@
     def tables(i):
         rs = span(i, rows)
         row = pos_ref[pl.ds(i, 1), :]
-        pos_out[i] = row
         col = jnp.transpose(jnp.broadcast_to(row.astype(F32), (HEAD, rows)))
-        pcol_out[rs, :] = col
+        pcol[rs, :] = col
         ang = col * freq_ref[...]
         lane = lax.broadcasted_iota(jnp.int32, (rows, HEAD), 1)
         cos_ref[rs, :] = jnp.cos(ang)
@@ -606,8 +493,6 @@
     loop(0, mid_seq, kv_proj)
     advance(1, 2)
     loop(mid_seq, n_seq, kv_proj)
-    kvo_out = pltpu.make_async_copy(kvo, kvo_hbm, out_sem.at[1])
-    kvo_out.start()
     advance(2, 1)
     settle(1)
     wf_out = pltpu.make_async_copy(wo, wf_hbm, out_sem.at[3])
@@ -626,34 +511,90 @@
                 q[rs, lanes(half * (hq // HEAD) + h)] = rope(res[:, lanes(h)], cos_ref[rs, :], sin_ref[rs, :]).astype(BF16)
         return body
 
-    def q_out(half):
-        hc = slice(half * hq, (half + 1) * hq)
-        return pltpu.make_async_copy(q.at[:, hc], q_hbm.at[:, hc], out_sem.at[7 + half])
+    def dkv_copy(t):
+        return pltpu.make_async_remote_copy(snd.at[t], rcv.at[t], dkv_send.at[t], dkv_recv.at[t],
+                                            device_id=peers['z'], device_id_type=MESH)
+
+    def blk_out(g, i):
+        rs, hc = span(i, rows), pl.ds(g * gsize * HEAD, gsize * HEAD)
+        return [pltpu.make_async_copy(src.at[rs, hc], dst.at[rs, hc], blk_sem.at[j, g * n_seq + i])
+                for j, (src, dst) in enumerate(((dy, o_hbm), (x, dq_hbm)))]
+
+    def attend(g):
+        def body(i):
+            if g == 0:
+                kv_copy(i).wait()
+            rs = span(i, rows)
+            pq = pcol[rs, :]
+            for j, ref in enumerate((pos_ref, px)):
+                key = ref[pl.ds(i, 1), :].astype(F32)
+                for b in range(rows // HEAD):
+                    mask[:, lanes(j * (rows // HEAD) + b)] = jnp.where(key[:, lanes(b)] <= pq, 0.0, NEG)
+            cos2, sin2 = cos_ref[rs, :], sin_ref[rs, :]
+            k = jnp.concatenate([kvo[i, :, lanes(2 * g)], kvx[i, :, lanes(2 * g)]], axis=0)
+            v = jnp.concatenate([kvo[i, :, lanes(2 * g + 1)], kvx[i, :, lanes(2 * g + 1)]], axis=0)
+            heads = [lanes(g * gsize + h) for h in range(gsize)]
+            for h, hc in enumerate(heads):
+                hrow = slice(h * rows, (h + 1) * rows)
+                qh, doh = q[rs, hc], do[rs, hc]
+                s = dot(qh, k, NT) * (SCALE * LOG2E) + mask[...]
+                m = jnp.max(s, axis=1, keepdims=True)
+                e = jnp.exp2(s - m)
+                rl = 1.0 / jnp.sum(e, axis=1, keepdims=True)
+                o = (dot(e.astype(BF16), v) * rl).astype(BF16)
+                dy[rs, hc] = o
+                delta = jnp.sum(doh.astype(F32) * o.astype(F32), axis=1, keepdims=True)
+                p = e * rl
+                p_s[hrow, :] = p.astype(BF16)
+                ds = (p * (dot(doh, v, NT) - delta)).astype(BF16)
+                ds_s[hrow, :] = ds
+                x[rs, hc] = unrope(dot(ds, k) * SCALE, cos2, sin2).astype(BF16)
+            do6 = jnp.concatenate([do[rs, hc] for hc in heads], axis=0)
+            q6 = jnp.concatenate([q[rs, hc] for hc in heads], axis=0)
+            dk = dot(ds_s[...], q6, TN) * SCALE
+            dv = dot(p_s[...], do6, TN)
+            t = g * n_seq + i
+            for j, val in enumerate((dk, dv)):
+                mine_kv[t, :, lanes(j)] = val[:rows]
+                snd[t, :, lanes(j)] = val[rows:]
+            dkv_copy(t).start()
+            for c in blk_out(g, i):
+                c.start()
+        return body
+
+    def finish(g):
+        def body(i):
+            t = g * n_seq + i
+            rs = span(i, rows)
+            dkv_copy(t).wait()
+            tot = mine_kv[t] + rcv[t]
+            dkv_out[rs, lanes(2 * g)] = unrope(tot[:, :HEAD], cos_ref[rs, :], sin_ref[rs, :]).astype(BF16)
+            dkv_out[rs, lanes(2 * g + 1)] = tot[:, HEAD:].astype(BF16)
+            for c in blk_out(g, i):
+                c.wait()
+        return body
 
     loop(0, mid_seq, do_proj)
     advance(3, 1)
     advance(2, 2)
     loop(mid_seq, n_seq, do_proj)
-    do_out = pltpu.make_async_copy(do, do_hbm, out_sem.at[2])
-    do_out.start()
     settle(2)
     wa_out = pltpu.make_async_copy(wa, wa_hbm, out_sem.at[5])
     wa_out.start()
     loop(0, n_seq, q_proj(0))
-    q_out(0).start()
+    px_copy().wait()
+    loop(0, mid_seq, attend(0))
     advance(3, 2)
+    loop(mid_seq, n_seq, attend(0))
     settle(3)
-    wb_out = pltpu.make_async_copy(wb, wb_hbm, out_sem.at[9])
+    wb_out = pltpu.make_async_copy(wb, wb_hbm, out_sem.at[1])
     wb_out.start()
     loop(0, n_seq, q_proj(1))
-    q_out(1).start()
-    px_copy().wait()
-    for i in range(n_seq):
-        px_out[i] = px[i:i + 1, :]
-        kv_copy(i).wait()
-    kvx_out = pltpu.make_async_copy(kvx, kvx_hbm, out_sem.at[6])
-    kvx_out.start()
-    for c in (r_out, kvo_out, do_out, wf_out, wkv_out, wa_out, wb_out, q_out(0), q_out(1), kvx_out):
+    for g in range(1, groups):
+        loop(0, n_seq, attend(g))
+    for g in range(groups):
+        loop(0, n_seq, finish(g))
+    for c in (r_out, wf_out, wkv_out, wa_out, wb_out):
         c.wait()
 
 
@@ -662,6 +603,7 @@
     n_seq, rows = pos.shape
     n_kv = wk.shape[1]
     shard = dim // 16
+    steps = n_seq * n_kv // HEAD
     half = HEAD // 2
     freq = np.float32(THETA) ** (-np.arange(half, dtype=np.float32) / half)
     freq = jnp.asarray(np.tile(freq, 2)[None])
@@ -674,10 +616,9 @@
     return pl.pallas_call(
         functools.partial(gather_kernel, (n_seq, rows, dim, n_kv)),
         in_specs=[hbm] * 6 + [vm] * 3,
-        out_specs=[hbm] * 9 + [vm] * 6,
-        out_shape=[sds((tokens, dim), BF16)] * 3 + [sds((n_seq, rows, 2 * n_kv), BF16)] * 2 + [
-            sds(w, BF16) for w in wshapes] + [sds((tokens, HEAD), F32)] * 2 + [
-            sds((1, dim), F32), sds((tokens, HEAD), F32)] + [sds((n_seq, 1, rows), jnp.int32)] * 2,
+        out_specs=[hbm] * 7 + [vm] * 2,
+        out_shape=[sds((tokens, dim), BF16)] * 3 + [sds(w, BF16) for w in wshapes] + [
+            sds((1, dim), F32), sds((tokens, 2 * n_kv), BF16)],
         scratch_shapes=[pltpu.VMEM((tokens, dim), BF16)] * 5 + [
             pltpu.VMEM((n_seq, rows, 2 * n_kv), BF16),
             pltpu.VMEM((n_seq, rows, 2 * n_kv), BF16),
@@ -685,10 +626,14 @@
             pltpu.VMEM((2, 2, 2, 2, 1, HEAD), F32),
             pltpu.VMEM((8, dim), F32),
             pltpu.VMEM((n_seq, rows), jnp.int32),
-            dma((6 * n_kv // HEAD + 5 + 2 * len(SLIM),)), dma((10,)), *[dma((4, 3, 3))] * 4,
-            *[dma((4,))] * 4, *[dma((n_seq + 1,))] * 2,
+            *[pltpu.VMEM((tokens, HEAD), F32)] * 3,
+            pltpu.VMEM((rows, 2 * rows), F32),
+            *[pltpu.VMEM((dim // n_kv * rows, 2 * rows), BF16)] * 2,
+            *[pltpu.VMEM((steps, rows, 2 * HEAD), F32)] * 3,
+            dma((6 * n_kv // HEAD + 5 + 2 * len(SLIM),)), dma((6,)), dma((2, steps)), *[dma((4, 3, 3))] * 4,
+            *[dma((4,))] * 4, *[dma((n_seq + 1,))] * 2, *[dma((steps,))] * 2,
         ],
-        compiler_params=pltpu.CompilerParams(collective_id=2, has_side_effects=True, vmem_limit_bytes=60 * 2 ** 20),
+        compiler_params=pltpu.CompilerParams(collective_id=2, has_side_effects=True, vmem_limit_bytes=63 * 2 ** 20),
         cost_estimate=pl.CostEstimate(flops=2 * tokens * dim * (2 * dim + 2 * n_kv), bytes_accessed=40 * 2 ** 20,
                                       transcendentals=0),
     )(x, dy, wq, wk, wv, wo, gain[None], pos, freq)
@@ -705,10 +650,9 @@
         groups = n_kv // HEAD
         x16 = hidden.reshape(tokens, dim)
         dy = grad_out.reshape(tokens, dim)
-        q, do, r, kv, kv_oth, w_kv, w_a, w_b, w_o, cos2, sin2, gain, pcol, pos, pos_oth = gather_project(
+        r, o, dq, w_kv, w_a, w_b, w_o, gain, dkv = gather_project(
             x16, dy, w_query, w_key, w_value, w_out, norm_gain, tok_pos)
         w_a, w_b, w_kv, w_o = (w.reshape(dim, -1) for w in (w_a, w_b, w_kv, w_o))
-        o, dq, dkv = attention(q, do, kv.reshape(tokens, -1), kv_oth.reshape(tokens, -1), pcol, pos, pos_oth, cos2, sin2)
         g_wq, g_wk, g_wv, g_wo, gg, result, grad_hidden = wgrad(o, dy, r, dq, dkv, x16, w_o, w_a, w_b, w_kv, gain)
         shard = lax.axis_index('fsdp') * cp_size + lax.axis_index('cp')
         g_gain = lax.dynamic_slice(gg[0], (shard * norm_gain.shape[0],), norm_gain.shape)

time: 251 us -> 240 us (0.956)
  Pallas kernels: 238 us -> 228 us
    pallas_call x1 -> x0, Pallas kernels: 78.5 us -> none  [attention(): pl.pallas_call(functools.partial(attn_kernel, n_seq, rows, groups, gsize)...]
    pallas_call x1, Pallas kernels: 70.6 us -> 137 us  [gather_project(): pl.pallas_call(functools.partial(gather_kernel, (n_seq, rows, dim, n_kv))...]
where the time goes in v3:
time: 240 us
  Pallas kernels  228 us (95%)
  local copies, waits for them, and re-layouts  11.6 us (5%)
    pallas_call x1, Pallas kernels, gather_project(): pl.pallas_call(functools.partial(gather_kernel, (n_seq, rows, dim, n_kv))...  137 us
    pallas_call x1, Pallas kernels, wgrad(): pl.pallas_call(functools.partial(wgrad_kernel, (tokens, dim, width, sub))...  90.6 us
    unnamed x16, local copies, waits for them, and re-layouts  10.3 us

profile of v3, /device:TPU:0, one launch (start us, length us, event | category | flops | bytes accessed | tf_op | source)
XLA Modules:
  0.0 240.0 jit_solution(7833526066407694248)
XLA Ops:
  0.6 137.1 %shard_map.144 = (bf16[1536,1536]{1,0:T(8,128)(2,1)}, bf16[1536,1536]{1,0:T(8,128)(2,1)}, bf16[1536,1536]{1,0:T(8,128)(2,1)}, bf16[2,2,2,2,3,32,512]{6,5,4,3,2,1...) custom-call(bf16[1536,1536]{1,0:T(8,128)(2,1)} %bitcast.13, ...), custom_call_target="tpu_custom_call" | custom-call | flops 16911433728 | bytes 41943040 | tf_op jit(solution)/shard_map/pallas_call | solution.py:616
  137.8 90.6 %shard_map.145 = (f32[96,1536]{1,0:T(8,128)}, f32[96,256]{1,0:T(8,128)}, f32[96,256]{1,0:T(8,128)}, f32[96,1536]{1,0:T(8,128)}, f32[1,1536]{1,0:T(1,128)}, /*ind...) custom-call(bf16[1536,1536]{1,0:T(8,128)(2,1)} %get-tuple-element.23.o_hbm, bf16[1536,1536]{1,0:T(8,128)(2,1)} %bitcast.16, ...), custom_call_target="tpu_custom_call" | custom-call | flops 16911433728 | bytes 31457280 | tf_op jit(solution)/shard_map/pallas_call | solution.py:287
  228.4 1.3 dynamic-slice_bitcast_fusion
  229.7 0.0 copy-start
  229.7 5.2 %copy.22 = bf16[6,256,1536]{2,1,0:T(8,128)(2,1)} copy(bf16[6,256,1536]{2,1,0:T(8,128)(2,1)} %bitcast.12) | data formatting | bytes 9437184
  234.9 0.0 copy-done
  234.9 0.0 copy-start.2
  234.9 0.0 copy-start.4
  234.9 0.0 copy-start.3
  234.9 0.0 copy-start.1
  234.9 2.2 copy.23
  237.1 0.0 copy-done.2
  237.1 0.8 copy.24
  237.9 0.0 copy-done.4
  237.9 0.6 copy.25
  238.6 0.0 copy-done.3
  238.6 0.6 copy.26
  239.2 0.0 copy-done.1
  239.2 0.8 copy.27
Async XLA Ops:
  229.7 5.2 %copy-start = (bf16[1536,1536]{1,0:T(8,128)(2,1)S(1)}, bf16[1536,1536]{1,0:T(8,128)(2,1)}, u32[]{:S(2)}) copy-start(bf16[1536,1536]{1,0:T(8,128)(2,1)} %get-tuple-element.33) | copy-start | bytes 14155780
  234.9 2.2 copy-start.2
  234.9 3.0 %copy-start.4 = (f32[96,256]{1,0:T(8,128)S(1)}, f32[96,256]{1,0:T(8,128)}, u32[]{:S(2)}) copy-start(f32[96,256]{1,0:T(8,128)} %get-tuple-element.49) | copy-start | bytes 294916
  234.9 3.7 %copy-start.3 = (f32[96,256]{1,0:T(8,128)S(1)}, f32[96,256]{1,0:T(8,128)}, u32[]{:S(2)}) copy-start(f32[96,256]{1,0:T(8,128)} %get-tuple-element.50) | copy-start | bytes 294916
  234.9 4.3 %copy-start.1 = (f32[96,1536]{1,0:T(8,128)S(1)}, f32[96,1536]{1,0:T(8,128)}, u32[]{:S(2)}) copy-start(f32[96,1536]{1,0:T(8,128)} %get-tuple-element.51) | copy-start | bytes 1769476

commit v4 on v3

--- a/solution.py
+++ b/solution.py
@@ -35,12 +35,24 @@
     lax.fori_loop(lo, hi, run, None)
 
 
+def total(a):
+    return jnp.sum(a, axis=1, keepdims=True)
+
+
+def average(a):
+    return jnp.mean(a, axis=1, keepdims=True)
+
+
 def span(i, size):
     return pl.ds(pl.multiple_of(i * size, size), size)
 
 
+def span_of(i, size):
+    return slice(i * size, (i + 1) * size)
+
+
 def lanes(i):
-    return slice(i * HEAD, (i + 1) * HEAD)
+    return span_of(i, HEAD)
 
 
 def rope(v, cos2, sin2):
@@ -54,6 +66,7 @@
 COLORS = ('xyz', 'yzx', 'zxy')
 SLIM = ('zxy', 'zyx')
 BLOCK = 256
+EARLY = 256
 
 
 def place():
@@ -76,13 +89,13 @@
     half = width // 2
     out = [('o', 0, half), ('o', half, half)]
     out += [('o', c, width) for c in range(width, dim, width)]
-    out += [('q', c, width) for c in range(0, dim, width)]
+    out += [('q', dim // 2, half), ('q', dim - width, width)]
     return out + [('kv', 0, half), ('kv', half, half)]
 
 
-def wgrad_kernel(shapes, o_hbm, dy_hbm, r_hbm, dq_hbm, dkv_hbm, x_hbm, wo_hbm, wa_hbm, wb_hbm, wkv_hbm, gain_ref,
+def wgrad_kernel(shapes, o_hbm, dy_hbm, r_hbm, dq_hbm, dkv_hbm, x_hbm, wo_hbm, wa_hbm, wb_hbm, wkv_hbm, gain_ref, part_ref,
                  gwq_ref, gwk_ref, gwv_ref, gwo_ref, gg_ref, res_hbm, gh_hbm,
-                 lhs, rhs, g, rcv_a, gain_rcv, wo, wkv, xb, dyb, dqb, dkvb, outb,
+                 lhs, rhs, g, rcv_a, part_rcv, part_sem, gain_rcv, wo, wkv, xb, dyb, dqb, dkvb, outb,
                  load_sem, w_sem, blk_sem, out_sem, *rest):
     tokens, dim, width, sub = shapes
     bits, peers = place()
@@ -148,12 +161,12 @@
 
     def dr_body(b):
         xf = xb[b % 2].astype(F32)
-        inv = lax.rsqrt(jnp.mean(xf * xf, axis=1, keepdims=True) + EPS)
+        inv = lax.rsqrt(average(xf * xf) + EPS)
         xh = xf * inv
         dr = dot(dqb[b % 2], lhs[0], NT) + dot(dkvb[b % 2], wkv[...], NT)
         gg_ref[...] = gg_ref[...] + jnp.sum(dr * xh, axis=0, keepdims=True)
         a = dr * gain_ref[...]
-        gx = inv * (a - xh * jnp.mean(a * xh, axis=1, keepdims=True))
+        gx = inv * (a - xh * average(a * xh))
         return (dyb[b % 2].astype(F32) + gx).astype(BF16)
 
     for c in blk_loads(0, (0,)):
@@ -197,14 +210,11 @@
     def fold(t):
         w = chunks[t][2]
         d2d(t).wait()
-        for y in range(2):
-            for x in range(2):
-                for z in range(2):
-                    at = {'y': y, 'x': x, 'z': z}
-                    for c in range(3):
-                        a1, a2, a3 = (at[a] for a in COLORS[c])
-                        rows = slice(z * 3 * sub + c * sub, z * 3 * sub + (c + 1) * sub)
-                        h[t][c, a1 * 4 + a2 * 2 + a3] = g[t % 2, y * 2 + x, core, rows, :w] + rcv_a[t % 2, y * 2 + x, rows, :w]
+        for y, x, z, c in np.ndindex(2, 2, 2, 3):
+            at = {'y': y, 'x': x, 'z': z}
+            a1, a2, a3 = (at[a] for a in COLORS[c])
+            rows = span_of(z * 3 + c, sub)
+            h[t][c, a1 * 4 + a2 * 2 + a3] = g[t % 2, y * 2 + x, core, rows, :w] + rcv_a[t % 2, y * 2 + x, rows, :w]
         for c in range(3):
             ici(t, c, 0).start()
         if t + 2 < n:
@@ -221,7 +231,7 @@
                 ici(t, c, p + 1).start()
                 continue
             kind, col, w = chunks[t]
-            rws = slice(c * sub, (c + 1) * sub)
+            rws = span_of(c, sub)
             tot = h[t][c, k] + rcv[t][p][c, 0]
             if kind == 'kv':
                 for j in range(w // HEAD):
@@ -231,6 +241,9 @@
                 (gwo_ref if kind == 'o' else gwq_ref)[rws, col:col + w] = tot
 
     gg_ref[...] = jnp.zeros_like(gg_ref)
+    part_copy = pltpu.make_async_remote_copy(part_ref.at[1 - bits['z']], part_rcv, part_sem.at[0], part_sem.at[1],
+                                             device_id=peers['z'], device_id_type=MESH)
+    part_copy.start()
 
     def gain_copy(i):
         return pltpu.make_async_remote_copy(gg_ref, gain_rcv.at[i], gain_send.at[i], gain_recv.at[i],
@@ -256,6 +269,8 @@
                 w_loads[0].wait()
             blocks((i - 2) * fill, (i - 1) * fill, (0,), res_hbm, res_body)
             if i == 3:
+                part_copy.wait()
+                gwq_ref[:, :hd] = part_ref[bits['z']] + part_rcv[...]
                 flush(res_hbm)
                 for c in [*w_loads[2:], *blk_loads(0, every)]:
                     c.start()
@@ -274,7 +289,7 @@
                 gain_copy(i - 6).start()
 
 
-def wgrad(o, dy, r, dq, dkv, x, w_o, w_a, w_b, w_kv, gain):
+def wgrad(o, dy, r, dq, dkv, x, w_o, w_a, w_b, w_kv, gain, part):
     tokens, dim = o.shape
     width = dkv.shape[1]
     shard = dim // 16
@@ -286,7 +301,7 @@
     dma = pltpu.SemaphoreType.DMA
     return pl.pallas_call(
         functools.partial(wgrad_kernel, (tokens, dim, width, sub)),
-        in_specs=[hbm] * 10 + [vm],
+        in_specs=[hbm] * 10 + [vm] * 2,
         out_specs=[vm] * 5 + [hbm] * 2,
         out_shape=[jax.ShapeDtypeStruct(a, F32) for a in (
             (shard, dim), (shard, width // 2), (shard, width // 2), (shard, dim), (1, dim))] + [jax.ShapeDtypeStruct((tokens, dim), BF16)] * 2,
@@ -295,6 +310,7 @@
             pltpu.VMEM((2, tokens, width), BF16),
             pltpu.VMEM((2, 4, 2, dim // 8, width), F32),
             pltpu.VMEM((2, 4, dim // 8, width), F32),
+            pltpu.VMEM(part.shape[1:], F32), dma((2,)),
             pltpu.VMEM((4, 1, dim), F32),
             pltpu.VMEM((dim, dim), BF16),
             pltpu.VMEM((dim, width), BF16),
@@ -308,15 +324,16 @@
         compiler_params=pltpu.CompilerParams(collective_id=1, has_side_effects=True, vmem_limit_bytes=60 * 2 ** 20),
         cost_estimate=pl.CostEstimate(flops=2 * tokens * dim * (2 * dim + width), bytes_accessed=30 * 2 ** 20,
                                       transcendentals=0),
-    )(o, dy, r, dq, dkv, x, w_o, w_a, w_b, w_kv, gain)
+    )(o, dy, r, dq, dkv, x, w_o, w_a, w_b, w_kv, gain, part)
 
 
 def gather_kernel(shapes, x_hbm, dy_hbm, wq_hbm, wk_hbm, wv_hbm, wo_hbm, gain_ref, pos_ref, freq_ref,
-                  r_hbm, o_hbm, dq_hbm, wkv_hbm, wa_hbm, wb_hbm, wf_hbm, gain_out, dkv_out,
+                  r_hbm, o_hbm, dq_hbm, wkv_hbm, wa_hbm, wb_hbm, wf_hbm, gain_out, dkv_out, part_out,
                   x, dy, r, q, do, kvo, kvx, wkv, wa, wb, wo, gbuf, grow, px, cos_ref, sin_ref, pcol,
-                  mask, p_s, ds_s, mine_kv, snd, rcv,
+                  mask, p_s, ds_s, mine_kv, snd, rcv, eg, ercv, eh, er1, er2,
                   load_sem, out_sem, blk_sem, ici_send, ici_recv, fwd_send, fwd_recv, own_send, own_recv,
-                  g_send, g_recv, kv_send, kv_recv, dkv_send, dkv_recv):
+                  g_send, g_recv, kv_send, kv_recv, dkv_send, dkv_recv,
+                  ed_send, ed_recv, ei_send, ei_recv, credit):
     n_seq, rows, dim, n_kv = shapes
     bits, peers = place()
     by, bx, bc, bz = (bits[a] for a in 'yxcz')
@@ -341,15 +358,15 @@
     for c in range(3):
         for g in range(n_kv // HEAD):
             hc = slice(g * HEAD, (g + 1) * HEAD)
-            rws = slice(c * third, (c + 1) * third)
+            rws = span_of(c, third)
             for j, w_hbm in enumerate((wk_hbm, wv_hbm)):
                 oc = slice((2 * g + j) * HEAD, (2 * g + j + 1) * HEAD)
                 load(w_hbm.at[rws, hc], wkv.at[by, bx, bc, bz, c, :, oc])
     n_first = len(loads)
     for c in range(3):
-        load(wo_hbm.at[c * third:(c + 1) * third, :], wo.at[by, bx, bc, bz, c])
+        load(wo_hbm.at[span_of(c, third), :], wo.at[by, bx, bc, bz, c])
     for c in range(len(SLIM)):
-        rws = slice(c * mid, (c + 1) * mid)
+        rws = span_of(c, mid)
         load(wq_hbm.at[rws, :hq], wa.at[by, bx, bc, bz, c])
         load(wq_hbm.at[rws, hq:], wb.at[by, bx, bc, bz, c])
     n_all = len(loads)
@@ -417,6 +434,10 @@
         return pltpu.make_async_remote_copy(pos_ref, px, kv_send.at[n_seq], kv_recv.at[n_seq],
                                             device_id=peers['z'], device_id_type=MESH)
 
+    def hop(i):
+        gain_copy(i).wait()
+        gain_copy(i + 1).start()
+
     gain_copy(0).start()
     for i in range(n_first):
         loads[i].wait()
@@ -426,8 +447,7 @@
         loads[i].wait()
     for p in (1, 2, 3):
         begin(p)
-    gain_copy(0).wait()
-    gain_copy(1).start()
+    hop(0)
 
     def tables(i):
         rs = span(i, rows)
@@ -442,13 +462,11 @@
 
     mid_seq = n_seq // 2
     loop(0, mid_seq, tables)
-    gain_copy(1).wait()
-    gain_copy(2).start()
+    hop(1)
     advance(0, 0)
     advance(1, 0)
     loop(mid_seq, n_seq, tables)
-    gain_copy(2).wait()
-    gain_copy(3).start()
+    hop(2)
     advance(0, 1)
     advance(1, 1)
     gain_copy(3).wait()
@@ -456,11 +474,11 @@
     lane = lax.broadcasted_iota(jnp.int32, (8, HEAD), 1)
     for b in range(dim // HEAD):
         acc = jnp.zeros((8, HEAD), F32)
-        for sh in range(16):
+        for sh, at in enumerate(np.ndindex(2, 2, 2, 2)):
             lo = shard * sh - HEAD * b
             if lo >= HEAD or lo + shard <= 0:
                 continue
-            row = jnp.broadcast_to(gbuf[sh // 8, (sh // 4) % 2, (sh // 2) % 2, sh % 2], (8, HEAD))
+            row = jnp.broadcast_to(gbuf[at], (8, HEAD))
             row = pltpu.roll(row, lo % HEAD, 1) if lo % HEAD else row
             acc = jnp.where((lane >= lo) & (lane < lo + shard), row, acc)
         grow[:, b * HEAD:(b + 1) * HEAD] = acc
@@ -470,17 +488,22 @@
     def norm(i):
         rs = span(i, rows // 2)
         xf = x[rs, :].astype(F32)
-        inv = lax.rsqrt(jnp.mean(xf * xf, axis=1, keepdims=True) + EPS)
+        inv = lax.rsqrt(average(xf * xf) + EPS)
         r[rs, :] = (xf * inv * grow[0:1, :]).astype(BF16)
 
     loop(0, 2 * n_seq, norm)
-    r_out = pltpu.make_async_copy(r, r_hbm, out_sem.at[0])
-    r_out.start()
+    puts = []
+
+    def put(src, dst):
+        c = pltpu.make_async_copy(src, dst, out_sem.at[len(puts)])
+        c.start()
+        puts.append(c)
+
+    put(r, r_hbm)
     advance(0, 2)
     advance(3, 0)
     settle(0)
-    wkv_out = pltpu.make_async_copy(wkv, wkv_hbm, out_sem.at[4])
-    wkv_out.start()
+    put(wkv, wkv_hbm)
 
     def kv_proj(i):
         rs = span(i, rows)
@@ -495,8 +518,7 @@
     loop(mid_seq, n_seq, kv_proj)
     advance(2, 1)
     settle(1)
-    wf_out = pltpu.make_async_copy(wo, wf_hbm, out_sem.at[3])
-    wf_out.start()
+    put(wo, wf_hbm)
     loads[l_dy].wait()
 
     def do_proj(i):
@@ -531,19 +553,18 @@
                 for b in range(rows // HEAD):
                     mask[:, lanes(j * (rows // HEAD) + b)] = jnp.where(key[:, lanes(b)] <= pq, 0.0, NEG)
             cos2, sin2 = cos_ref[rs, :], sin_ref[rs, :]
-            k = jnp.concatenate([kvo[i, :, lanes(2 * g)], kvx[i, :, lanes(2 * g)]], axis=0)
-            v = jnp.concatenate([kvo[i, :, lanes(2 * g + 1)], kvx[i, :, lanes(2 * g + 1)]], axis=0)
+            k, v = (jnp.concatenate([kvo[i, :, lanes(j)], kvx[i, :, lanes(j)]], axis=0) for j in (2 * g, 2 * g + 1))
             heads = [lanes(g * gsize + h) for h in range(gsize)]
             for h, hc in enumerate(heads):
-                hrow = slice(h * rows, (h + 1) * rows)
+                hrow = span_of(h, rows)
                 qh, doh = q[rs, hc], do[rs, hc]
                 s = dot(qh, k, NT) * (SCALE * LOG2E) + mask[...]
                 m = jnp.max(s, axis=1, keepdims=True)
                 e = jnp.exp2(s - m)
-                rl = 1.0 / jnp.sum(e, axis=1, keepdims=True)
+                rl = 1.0 / total(e)
                 o = (dot(e.astype(BF16), v) * rl).astype(BF16)
                 dy[rs, hc] = o
-                delta = jnp.sum(doh.astype(F32) * o.astype(F32), axis=1, keepdims=True)
+                delta = total(doh.astype(F32) * o.astype(F32))
                 p = e * rl
                 p_s[hrow, :] = p.astype(BF16)
                 ds = (p * (dot(doh, v, NT) - delta)).astype(BF16)
@@ -562,6 +583,67 @@
                 c.start()
         return body
 
+    seg = dim // 4
+    early = ('xy', 'yx')
+
+    def e_swap(t):
+        return pltpu.make_async_remote_copy(eg.at[:, 1 - bc], ercv, ed_send.at[t], ed_recv.at[t],
+                                            device_id=peers['c'], device_id_type=MESH)
+
+    def e_ici(t, c, p):
+        b1, b2 = (bits[a] for a in early[c])
+        src = (eh.at[t, c, 1 - b1], eh.at[t, c, b1, 1 - b2])[p]
+        return pltpu.make_async_remote_copy(src, (er1, er2)[p].at[t, c], ei_send.at[t, c, p], ei_recv.at[t, c, p],
+                                            device_id=peers[early[c][p]], device_id_type=MESH)
+
+    def e_compute(t):
+        def body(yx):
+            res = dot(r[:, span(yx, seg)], x[:, span_of(t, EARLY)], TN)
+            eg[yx, 0] = res[:seg // 2]
+            eg[yx, 1] = res[seg // 2:]
+        loop(0, 4, body)
+        if t:
+            pl.semaphore_wait(credit, 1)
+        e_swap(t).start()
+
+    def e_fold(t):
+        e_swap(t).wait()
+        for yy, xx, zz, c in np.ndindex(2, 2, 2, 2):
+            rws = pl.ds(zz * shard + c * mid, mid)
+            i1, i2 = (yy, xx) if early[c] == 'yx' else (xx, yy)
+            eh[t, c, i1, i2, zz] = eg[yy * 2 + xx, bc, rws] + ercv[yy * 2 + xx, rws]
+        for c in range(2):
+            e_ici(t, c, 0).start()
+        if t + 1 < hq // EARLY:
+            pl.semaphore_signal(credit, inc=1, device_id=peers['c'], device_id_type=MESH)
+
+    def e_reduce(t, p):
+        for c in range(2):
+            b1, b2 = (bits[a] for a in early[c])
+            e_ici(t, c, p).wait()
+            if p == 0:
+                for j in range(2):
+                    eh[t, c, b1, j] = eh[t, c, b1, j] + er1[t, c, j]
+                e_ici(t, c, 1).start()
+            else:
+                part_out[:, span_of(c, mid), span_of(t, EARLY)] = eh[t, c, b1, b2] + er2[t, c]
+
+    def gap(k):
+        for p in (1, 0):
+            if 0 <= k - 2 - p < hq // EARLY:
+                e_reduce(k - 2 - p, p)
+        if 0 <= k - 1 < hq // EARLY:
+            e_fold(k - 1)
+        if k < hq // EARLY:
+            e_compute(k)
+
+    def second(i):
+        for k in range(hq // EARLY + 3):
+            @pl.when(i == k)
+            def _(k=k):
+                gap(k)
+        attend(1)(i)
+
     def finish(g):
         def body(i):
             t = g * n_seq + i
@@ -579,22 +661,26 @@
     advance(2, 2)
     loop(mid_seq, n_seq, do_proj)
     settle(2)
-    wa_out = pltpu.make_async_copy(wa, wa_hbm, out_sem.at[5])
-    wa_out.start()
+    put(wa, wa_hbm)
     loop(0, n_seq, q_proj(0))
     px_copy().wait()
-    loop(0, mid_seq, attend(0))
-    advance(3, 2)
-    loop(mid_seq, n_seq, attend(0))
+
+    def first(i):
+        attend(0)(i)
+
+        @pl.when(i == mid_seq - 1)
+        def _():
+            advance(3, 2)
+
+    loop(0, n_seq, first)
     settle(3)
-    wb_out = pltpu.make_async_copy(wb, wb_hbm, out_sem.at[1])
-    wb_out.start()
+    put(wb, wb_hbm)
     loop(0, n_seq, q_proj(1))
-    for g in range(1, groups):
-        loop(0, n_seq, attend(g))
+    assert groups == 2 and hq // EARLY + 3 <= n_seq and hq == gsize * HEAD
+    loop(0, n_seq, second)
     for g in range(groups):
         loop(0, n_seq, finish(g))
-    for c in (r_out, wf_out, wkv_out, wa_out, wb_out):
+    for c in puts:
         c.wait()
 
 
@@ -604,6 +690,7 @@
     n_kv = wk.shape[1]
     shard = dim // 16
     steps = n_seq * n_kv // HEAD
+    n_early = dim // 2 // EARLY
     half = HEAD // 2
     freq = np.float32(THETA) ** (-np.arange(half, dtype=np.float32) / half)
     freq = jnp.asarray(np.tile(freq, 2)[None])
@@ -616,9 +703,9 @@
     return pl.pallas_call(
         functools.partial(gather_kernel, (n_seq, rows, dim, n_kv)),
         in_specs=[hbm] * 6 + [vm] * 3,
-        out_specs=[hbm] * 7 + [vm] * 2,
+        out_specs=[hbm] * 7 + [vm] * 3,
         out_shape=[sds((tokens, dim), BF16)] * 3 + [sds(w, BF16) for w in wshapes] + [
-            sds((1, dim), F32), sds((tokens, 2 * n_kv), BF16)],
+            sds((1, dim), F32), sds((tokens, 2 * n_kv), BF16), sds((2, shard, dim // 2), F32)],
         scratch_shapes=[pltpu.VMEM((tokens, dim), BF16)] * 5 + [
             pltpu.VMEM((n_seq, rows, 2 * n_kv), BF16),
             pltpu.VMEM((n_seq, rows, 2 * n_kv), BF16),
@@ -630,10 +717,14 @@
             pltpu.VMEM((rows, 2 * rows), F32),
             *[pltpu.VMEM((dim // n_kv * rows, 2 * rows), BF16)] * 2,
             *[pltpu.VMEM((steps, rows, 2 * HEAD), F32)] * 3,
+            pltpu.VMEM((4, 2, dim // 8, EARLY), F32),
+            pltpu.VMEM((4, dim // 8, EARLY), F32),
+            *[pltpu.VMEM((n_early, 2) + k + (shard // 2, EARLY), F32) for k in ((2, 2, 2), (2, 2), (2,))],
             dma((6 * n_kv // HEAD + 5 + 2 * len(SLIM),)), dma((6,)), dma((2, steps)), *[dma((4, 3, 3))] * 4,
             *[dma((4,))] * 4, *[dma((n_seq + 1,))] * 2, *[dma((steps,))] * 2,
+            *[dma((n_early,))] * 2, *[dma((n_early, 2, 2))] * 2, pltpu.SemaphoreType.REGULAR,
         ],
-        compiler_params=pltpu.CompilerParams(collective_id=2, has_side_effects=True, vmem_limit_bytes=63 * 2 ** 20),
+        compiler_params=pltpu.CompilerParams(collective_id=2, has_side_effects=True, vmem_limit_bytes=67043328),
         cost_estimate=pl.CostEstimate(flops=2 * tokens * dim * (2 * dim + 2 * n_kv), bytes_accessed=40 * 2 ** 20,
                                       transcendentals=0),
     )(x, dy, wq, wk, wv, wo, gain[None], pos, freq)
@@ -650,10 +741,10 @@
         groups = n_kv // HEAD
         x16 = hidden.reshape(tokens, dim)
         dy = grad_out.reshape(tokens, dim)
-        r, o, dq, w_kv, w_a, w_b, w_o, gain, dkv = gather_project(
+        r, o, dq, w_kv, w_a, w_b, w_o, gain, dkv, part = gather_project(
             x16, dy, w_query, w_key, w_value, w_out, norm_gain, tok_pos)
         w_a, w_b, w_kv, w_o = (w.reshape(dim, -1) for w in (w_a, w_b, w_kv, w_o))
-        g_wq, g_wk, g_wv, g_wo, gg, result, grad_hidden = wgrad(o, dy, r, dq, dkv, x16, w_o, w_a, w_b, w_kv, gain)
+        g_wq, g_wk, g_wv, g_wo, gg, result, grad_hidden = wgrad(o, dy, r, dq, dkv, x16, w_o, w_a, w_b, w_kv, gain, part)
         shard = lax.axis_index('fsdp') * cp_size + lax.axis_index('cp')
         g_gain = lax.dynamic_slice(gg[0], (shard * norm_gain.shape[0],), norm_gain.shape)
         return result.reshape(hidden.shape), grad_hidden.reshape(hidden.shape), g_wq, g_wk, g_wv, g_wo, g_gain

time: 240 us -> 226 us (0.942)
  Pallas kernels: 228 us -> 213 us
    pallas_call x1, Pallas kernels: 90.6 us -> 74.5 us  [wgrad(): pl.pallas_call(functools.partial(wgrad_kernel, (tokens, dim, width, sub))...]
where the time goes in v4:
time: 226 us; the launch traced here: 225 us
  Pallas kernels  213 us (94%)
  local copies, waits for them, and re-layouts  11.6 us (5%)
    pallas_call x1, Pallas kernels, gather_project(): pl.pallas_call(functools.partial(gather_kernel, (n_seq, rows, dim, n_kv))...  138 us
    pallas_call x1, Pallas kernels, wgrad(): pl.pallas_call(functools.partial(wgrad_kernel, (tokens, dim, width, sub))...  74.5 us
    unnamed x16, local copies, waits for them, and re-layouts  10.3 us

profile of v4, /device:TPU:0, one launch (start us, length us, event | category | flops | bytes accessed | tf_op | source)
XLA Modules:
  0.0 225.3 jit_solution(1181251621776972242)
XLA Ops:
  0.6 138.5 %shard_map.144 = (bf16[1536,1536]{1,0:T(8,128)(2,1)}, bf16[1536,1536]{1,0:T(8,128)(2,1)}, bf16[1536,1536]{1,0:T(8,128)(2,1)}, bf16[2,2,2,2,3,32,512]{6,5,4,3,2,1...) custom-call(bf16[1536,1536]{1,0:T(8,128)(2,1)} %bitcast.13, ...), custom_call_target="tpu_custom_call" | custom-call | flops 16911433728 | bytes 41943040 | tf_op jit(solution)/shard_map/pallas_call | solution.py:703
  139.1 74.5 %shard_map.145 = (f32[96,1536]{1,0:T(8,128)}, f32[96,256]{1,0:T(8,128)}, f32[96,256]{1,0:T(8,128)}, f32[96,1536]{1,0:T(8,128)}, f32[1,1536]{1,0:T(1,128)}, /*ind...) custom-call(bf16[1536,1536]{1,0:T(8,128)(2,1)} %get-tuple-element.24.o_hbm, bf16[1536,1536]{1,0:T(8,128)(2,1)} %bitcast.16, ...), custom_call_target="tpu_custom_call" | custom-call | flops 16911433728 | bytes 31457280 | tf_op jit(solution)/shard_map/pallas_call | solution.py:302
  213.6 1.3 dynamic-slice_bitcast_fusion
  214.9 0.0 copy-start
  214.9 5.2 %copy.22 = bf16[6,256,1536]{2,1,0:T(8,128)(2,1)} copy(bf16[6,256,1536]{2,1,0:T(8,128)(2,1)} %bitcast.12) | data formatting | bytes 9437184
  220.1 0.0 copy-done
  220.1 0.0 copy-start.2
  220.1 0.0 copy-start.4
  220.1 0.0 copy-start.3
  220.1 0.0 copy-start.1
  220.2 2.2 copy.23
  222.3 0.0 copy-done.2
  222.3 0.8 copy.24
  223.2 0.0 copy-done.4
  223.2 0.6 copy.25
  223.8 0.0 copy-done.3
  223.8 0.6 copy.26
  224.4 0.0 copy-done.1
  224.5 0.8 copy.27
Async XLA Ops:
  214.9 5.2 %copy-start = (bf16[1536,1536]{1,0:T(8,128)(2,1)S(1)}, bf16[1536,1536]{1,0:T(8,128)(2,1)}, u32[]{:S(2)}) copy-start(bf16[1536,1536]{1,0:T(8,128)(2,1)} %get-tuple-element.35) | copy-start | bytes 14155780
  220.1 2.2 copy-start.2
  220.1 3.0 %copy-start.4 = (f32[96,256]{1,0:T(8,128)S(1)}, f32[96,256]{1,0:T(8,128)}, u32[]{:S(2)}) copy-start(f32[96,256]{1,0:T(8,128)} %get-tuple-element.51) | copy-start | bytes 294916
  220.1 3.7 %copy-start.3 = (f32[96,256]{1,0:T(8,128)S(1)}, f32[96,256]{1,0:T(8,128)}, u32[]{:S(2)}) copy-start(f32[96,256]{1,0:T(8,128)} %get-tuple-element.52) | copy-start | bytes 294916
  220.1 4.3 %copy-start.1 = (f32[96,1536]{1,0:T(8,128)S(1)}, f32[96,1536]{1,0:T(8,128)}, u32[]{:S(2)}) copy-start(f32[96,1536]{1,0:T(8,128)} %get-tuple-element.53) | copy-start | bytes 1769476

commit v5 on v4

--- a/solution.py
+++ b/solution.py
@@ -255,7 +255,6 @@
 
     every = (0, 1, 2, 3)
     third, fill = n_blk // 3, n_blk // 2
-    assert [c[0] for c in chunks].count('o') == 4
     for i in range(n + 4):
         if i < n:
             compute(i)
@@ -555,10 +554,18 @@
             cos2, sin2 = cos_ref[rs, :], sin_ref[rs, :]
             k, v = (jnp.concatenate([kvo[i, :, lanes(j)], kvx[i, :, lanes(j)]], axis=0) for j in (2 * g, 2 * g + 1))
             heads = [lanes(g * gsize + h) for h in range(gsize)]
+
+            def products(hc):
+                return dot(q[rs, hc], k, NT), dot(do[rs, hc], v, NT)
+
+            coming = products(heads[0])
             for h, hc in enumerate(heads):
                 hrow = span_of(h, rows)
-                qh, doh = q[rs, hc], do[rs, hc]
-                s = dot(qh, k, NT) * (SCALE * LOG2E) + mask[...]
+                doh = do[rs, hc]
+                raw, dp = coming
+                s = raw * (SCALE * LOG2E) + mask[...]
+                if hc != heads[-1]:
+                    coming = products(heads[h + 1])
                 m = jnp.max(s, axis=1, keepdims=True)
                 e = jnp.exp2(s - m)
                 rl = 1.0 / total(e)
@@ -567,7 +574,7 @@
                 delta = total(doh.astype(F32) * o.astype(F32))
                 p = e * rl
                 p_s[hrow, :] = p.astype(BF16)
-                ds = (p * (dot(doh, v, NT) - delta)).astype(BF16)
+                ds = (p * (dp - delta)).astype(BF16)
                 ds_s[hrow, :] = ds
                 x[rs, hc] = unrope(dot(ds, k) * SCALE, cos2, sin2).astype(BF16)
             do6 = jnp.concatenate([do[rs, hc] for hc in heads], axis=0)

time: 226 us -> 226 us (level)
  no operation moved by 1% of the time
where the time goes in v5:
time: 226 us; the launch traced here: 225 us
  Pallas kernels  213 us (94%)
  local copies, waits for them, and re-layouts  11.6 us (5%)
    pallas_call x1, Pallas kernels, gather_project(): pl.pallas_call(functools.partial(gather_kernel, (n_seq, rows, dim, n_kv))...  138 us
    pallas_call x1, Pallas kernels, wgrad(): pl.pallas_call(functools.partial(wgrad_kernel, (tokens, dim, width, sub))...  75.4 us
    unnamed x16, local copies, waits for them, and re-layouts  10.3 us

profile of v5, /device:TPU:0, one launch (start us, length us, event | category | flops | bytes accessed | tf_op | source)
XLA Modules:
  0.0 225.3 jit_solution(2216013101127069185)
XLA Ops:
  0.6 137.6 %shard_map.144 = (bf16[1536,1536]{1,0:T(8,128)(2,1)}, bf16[1536,1536]{1,0:T(8,128)(2,1)}, bf16[1536,1536]{1,0:T(8,128)(2,1)}, bf16[2,2,2,2,3,32,512]{6,5,4,3,2,1...) custom-call(bf16[1536,1536]{1,0:T(8,128)(2,1)} %bitcast.13, ...), custom_call_target="tpu_custom_call" | custom-call | flops 16911433728 | bytes 41943040 | tf_op jit(solution)/shard_map/pallas_call | solution.py:710
  138.3 75.4 %shard_map.145 = (f32[96,1536]{1,0:T(8,128)}, f32[96,256]{1,0:T(8,128)}, f32[96,256]{1,0:T(8,128)}, f32[96,1536]{1,0:T(8,128)}, f32[1,1536]{1,0:T(1,128)}, /*ind...) custom-call(bf16[1536,1536]{1,0:T(8,128)(2,1)} %get-tuple-element.24.o_hbm, bf16[1536,1536]{1,0:T(8,128)(2,1)} %bitcast.16, ...), custom_call_target="tpu_custom_call" | custom-call | flops 16911433728 | bytes 31457280 | tf_op jit(solution)/shard_map/pallas_call | solution.py:301
  213.6 1.3 dynamic-slice_bitcast_fusion
  214.9 0.0 copy-start
  214.9 5.2 %copy.22 = bf16[6,256,1536]{2,1,0:T(8,128)(2,1)} copy(bf16[6,256,1536]{2,1,0:T(8,128)(2,1)} %bitcast.12) | data formatting | bytes 9437184
  220.1 0.0 copy-done
  220.1 0.0 copy-start.2
  220.1 0.0 copy-start.4
  220.1 0.0 copy-start.3
  220.1 0.0 copy-start.1
  220.2 2.2 copy.23
  222.3 0.0 copy-done.2
  222.3 0.8 copy.24
  223.2 0.0 copy-done.4
  223.2 0.6 copy.25
  223.8 0.0 copy-done.3
  223.8 0.6 copy.26
  224.4 0.0 copy-done.1
  224.5 0.8 copy.27
Async XLA Ops:
  214.9 5.2 %copy-start = (bf16[1536,1536]{1,0:T(8,128)(2,1)S(1)}, bf16[1536,1536]{1,0:T(8,128)(2,1)}, u32[]{:S(2)}) copy-start(bf16[1536,1536]{1,0:T(8,128)(2,1)} %get-tuple-element.35) | copy-start | bytes 14155780
  220.1 2.2 copy-start.2
  220.1 3.0 %copy-start.4 = (f32[96,256]{1,0:T(8,128)S(1)}, f32[96,256]{1,0:T(8,128)}, u32[]{:S(2)}) copy-start(f32[96,256]{1,0:T(8,128)} %get-tuple-element.51) | copy-start | bytes 294916
  220.1 3.7 %copy-start.3 = (f32[96,256]{1,0:T(8,128)S(1)}, f32[96,256]{1,0:T(8,128)}, u32[]{:S(2)}) copy-start(f32[96,256]{1,0:T(8,128)} %get-tuple-element.52) | copy-start | bytes 294916
  220.1 4.3 %copy-start.1 = (f32[96,1536]{1,0:T(8,128)S(1)}, f32[96,1536]{1,0:T(8,128)}, u32[]{:S(2)}) copy-start(f32[96,1536]{1,0:T(8,128)} %get-tuple-element.53) | copy-start | bytes 1769476
